TPU v7x, 32 devices: a whole 2x2x4 slice. The times are simulated.
32 devices in a mesh: section: 4 (over x, core), ep: 8 (over z, y).
Axes of the slice: x: 2, y: 2, z: 4, core: 2. Of those that a mesh axis runs over, the one named last changes fastest.
Arguments:
- output_grad: bfloat16 [4, 2048, 1024], P('section', 'ep'), may hold values from -6 to 6
- layer_input: bfloat16 [4, 2048, 1024], P('section', 'ep'), may hold values from -6 to 6
- expert_ids: int32 [4, 2048, 8], P('section', 'ep'), may hold values from 0 to 31, all different within a row; in each aligned block of 256 rows (0 to 255, 256 to 511, ..., all dimensions but the last counted through in order) at most 80 rows name the same one
- route_probs: bfloat16 [4, 2048, 8], P('section', 'ep'), may hold values from 0.049804688 to 0.44921875
- gate_weight: bfloat16 [4, 32, 1024, 384], P('section', 'ep'), may hold values from -0.1875 to 0.1875
- up_weight: bfloat16 [4, 32, 1024, 384], P('section', 'ep'), may hold values from -0.1875 to 0.1875
- down_weight: bfloat16 [4, 32, 384, 1024], P('section', 'ep'), may hold values from -0.3125 to 0.3125
- saved_inputs: bfloat16 [4, 32, 640, 1024], P('section', 'ep'), may hold values from -6 to 6
- saved_gate_grad: bfloat16 [4, 32, 640, 384], P('section', 'ep'), may hold values from -0.5 to 0.5
- saved_up_grad: bfloat16 [4, 32, 640, 384], P('section', 'ep'), may hold values from -0.5 to 0.5
- saved_counts: int32 [4, 32, 8], P('section', 'ep'), may hold values from 0 to 80, as said below
Outputs:
- upstream_grad: bfloat16 [4, 2048, 1024], P('section', 'ep')
- prob_grad: bfloat16 [4, 2048, 8], P('section', 'ep')
- gate_weight_grad: bfloat16 [4, 32, 1024, 384], P('section', 'ep')
- up_weight_grad: bfloat16 [4, 32, 1024, 384], P('section', 'ep')
Inputs may be any that keep to these rules, and one draw needn't show every extreme that they name: `expert_ids`: each token names 8 different experts. Among the tokens of one device (aligned blocks of 256 tokens of a section) no expert is named more than 80 times, a bound that some block reaches. `saved_counts`: rows of a block at or beyond its count are padding; some block is full in every draw.
All inputs are finite; a program needn't handle non-finite values.
Results may differ from a plain program's by a relative error of at most 0.008.
Values may be sent and summed in bfloat16 or wider, within the bound.
A program may use at most 128 MiB of HBM per device.

v0:
```python
import jax
import jax.numpy as jnp
from jax import lax
from jax.sharding import PartitionSpec as P


def from_behind(array, axis, by):
    devices = lax.axis_size(axis)
    pairs = [(i, i + by) for i in range(devices) if 0 <= i + by < devices]
    return lax.ppermute(array, axis, pairs)


def expert_rows(grad_part, input_part, prob_part, w_gate, w_up, w_down):
    gate_pre = jnp.einsum("sepd,edf->sepf", input_part, w_gate, preferred_element_type=jnp.float32)
    up_pre = jnp.einsum("sepd,edf->sepf", input_part, w_up, preferred_element_type=jnp.float32)
    sigma = jax.nn.sigmoid(gate_pre)
    active = gate_pre * sigma
    hidden = (active * up_pre).astype(jnp.bfloat16)
    hidden_grad = jnp.einsum(
        "sepd,efd->sepf", grad_part, w_down, preferred_element_type=jnp.float32
    )
    slot_prob = jnp.sum(hidden_grad * hidden.astype(jnp.float32), axis=3)
    scaled = hidden_grad * prob_part.astype(jnp.float32)[..., None]
    gate_grad = (scaled * up_pre * sigma * (1.0 + gate_pre * (1.0 - sigma))).astype(jnp.bfloat16)
    up_grad = (scaled * active).astype(jnp.bfloat16)
    slot_grad = jnp.einsum("sepf,edf->sepd", gate_grad, w_gate, preferred_element_type=jnp.float32)
    slot_grad = slot_grad + jnp.einsum(
        "sepf,edf->sepd", up_grad, w_up, preferred_element_type=jnp.float32
    )
    return (slot_grad.astype(jnp.bfloat16), slot_prob.astype(jnp.bfloat16))


def per_device(
    output_grad,
    layer_input,
    expert_ids,
    route_probs,
    gate_weight,
    up_weight,
    down_weight,
    saved_inputs,
    saved_gate_grad,
    saved_up_grad,
    saved_counts,
):
    ep_count = lax.axis_size("ep")
    w_gate = gate_weight[0]
    w_up = up_weight[0]
    w_down = down_weight[0]
    local_experts = w_gate.shape[0]
    experts_all = local_experts * ep_count
    slots_all = saved_inputs.shape[2]
    capacity = slots_all // ep_count
    tok_rows = expert_ids.shape[1]
    top_count = expert_ids.shape[2]
    width = output_grad.shape[2]
    live = jnp.arange(capacity, dtype=jnp.int32)[None, None, :] < saved_counts[0][:, :, None]
    masked = (
        saved_inputs[0] * live.reshape(local_experts, slots_all).astype(jnp.bfloat16)[:, :, None]
    )
    gate_part = jnp.einsum(
        "esd,esf->edf", masked, saved_gate_grad[0], preferred_element_type=jnp.float32
    ).astype(jnp.bfloat16)
    up_part = jnp.einsum(
        "esd,esf->edf", masked, saved_up_grad[0], preferred_element_type=jnp.float32
    ).astype(jnp.bfloat16)
    flat_ids = expert_ids[0].reshape(-1)
    onehot = (flat_ids[:, None] == jnp.arange(experts_all, dtype=jnp.int32)[None, :]).astype(
        jnp.int32
    )
    before = jnp.cumsum(onehot, axis=0) - onehot
    block_slot = jnp.sum(before * onehot, axis=1)
    place = flat_ids * capacity + block_slot
    send_prob = (
        jnp.zeros((experts_all * capacity,), jnp.bfloat16).at[place].set(route_probs[0].reshape(-1))
    )
    send_prob = send_prob.reshape(ep_count, local_experts, capacity)
    grad_rows = jnp.broadcast_to(output_grad[0][:, None, :], (tok_rows, top_count, width)).reshape(
        -1, width
    )
    input_rows = jnp.broadcast_to(layer_input[0][:, None, :], (tok_rows, top_count, width)).reshape(
        -1, width
    )
    send_grad = jnp.zeros((experts_all * capacity, width), jnp.bfloat16).at[place].set(grad_rows)
    send_grad = send_grad.reshape(ep_count, local_experts, capacity, width)
    send_input = jnp.zeros((experts_all * capacity, width), jnp.bfloat16).at[place].set(input_rows)
    send_input = send_input.reshape(ep_count, local_experts, capacity, width)
    received = (
        lax.all_to_all(send_grad, "ep", split_axis=0, concat_axis=0, tiled=True),
        lax.all_to_all(send_input, "ep", split_axis=0, concat_axis=0, tiled=True),
        lax.all_to_all(send_prob, "ep", split_axis=0, concat_axis=0, tiled=True),
    )
    slot_grad, slot_prob = expert_rows(received[0], received[1], received[2], w_gate, w_up, w_down)
    returned = (
        lax.all_to_all(slot_grad, "ep", split_axis=0, concat_axis=0, tiled=True),
        lax.all_to_all(slot_prob, "ep", split_axis=0, concat_axis=0, tiled=True),
    )
    back_grad = returned[0].reshape(experts_all * capacity, width)
    picked = back_grad[place].reshape(tok_rows, top_count, width).astype(jnp.float32)
    input_grad = jnp.sum(picked, axis=1).astype(jnp.bfloat16)
    prob_part = returned[1].reshape(-1)[place].reshape(tok_rows, top_count)
    upstream = from_behind(input_grad[None], "section", -1)
    return (upstream, prob_part[None], gate_part[None], up_part[None])


def solution(mesh):
    return jax.shard_map(
        per_device,
        mesh=mesh,
        in_specs=(
            P("section", "ep", None),
            P("section", "ep", None),
            P("section", "ep", None),
            P("section", "ep", None),
            P("section", "ep", None, None),
            P("section", "ep", None, None),
            P("section", "ep", None, None),
            P("section", "ep", None, None),
            P("section", "ep", None, None),
            P("section", "ep", None, None),
            P("section", "ep", None),
        ),
        out_specs=(
            P("section", "ep", None),
            P("section", "ep", None),
            P("section", "ep", None, None),
            P("section", "ep", None, None),
        ),
        check_vma=False,
    )
```

profile of v0, /device:TPU:9, one launch (start us, length us, event | category | flops | bytes accessed | tf_op | source)
XLA Modules:
  0.0 523.1 jit_solution(5019810260614388898)
XLA Ops:
  0.6 0.0 copy-start
  0.6 1.0 copy.90
  1.6 0.1 eq.29
  1.7 0.1 eq.25
  1.8 0.7 broadcast_multiply_fusion
  2.6 0.7 fusion.43
  3.3 15.9 %reduce-window.6 = s32[32,16,128]{2,1,0:T(8,128)S(1)} reduce-window(s32[32,16,128]{2,1,0:T(8,128)} %fusion.43, s32[]{:T(128)} %constant.8.clone.1), window={size=1x1x128 pad=0_0x0_0x127_0}, to_apply=%region_0.0 | reduce-window | flops 8323072 | bytes 524292 | tf_op jit(solution)/shard_map/reduce-window
  19.2 0.8 slice.12
  20.0 1.2 copy.109
  21.2 0.2 reduce-window.9
  21.4 0.8 broadcast_add_fusion
  22.2 0.1 copy.89
  22.4 0.1 mul.61
  22.5 0.8 copy.95
  23.3 0.1 reshape.140
  23.4 1.1 fusion.42
  24.5 14.6 %scatter_custom_fusion.1 = bf16[2560]{0:T(1024)(128)(2,1)S(1)} fusion(s32[2048]{0:T(1024)S(1)} %bitcast.138, bf16[2048]{0:T(1024)(128)(2,1)S(1)} %reshape.140, bf16[]{:T(256)} %constant.6.clone.1), kind=kCustom, calls=%fused_computation.70 | custom fusion | bytes 5122 | tf_op jit(solution)/shard_map/scatter | solution.py:75
  39.1 0.7 reshape.106
  39.8 5.7 %all-to-all-start.1 = ((bf16[8,4,80]{2,1,0:T(4,128)(2,1)}), bf16[8,4,80]{2,1,0:T(4,128)(2,1)S(1)}, u32[]{:S(2)}, u32[]{:S(2)}) async-start(bf16[8,4,80]{2,1,0:T(4,128)(2,1)} %reshape.106), calls=%async_computation.1 | async-start | bytes 16384 | tf_op jit(solution)/shard_map/all_to_all | solution.py:91
  45.5 13.3 %scatter_custom_fusion.2 = bf16[2560,1024]{1,0:T(8,128)(2,1)} fusion(s32[2048]{0:T(1024)S(1)} %bitcast.139, bf16[]{:T(256)} %constant.6.clone.1, bf16[256,1024]{1,0:T(8,128)(2,1)} %bitcast.133), kind=kCustom, calls=%fused_computation.17 | custom fusion | bytes 5767170 | tf_op jit(solution)/shard_map/scatter | solution.py:86
  58.9 0.0 all-to-all-done.1
  58.9 17.3 %all-to-all-start.2 = ((bf16[8,4,80,1024]{3,2,1,0:T(8,128)(2,1)}), bf16[8,4,80,1024]{3,2,1,0:T(8,128)(2,1)}, u32[]{:S(2)}, u32[]{:S(2)}) async-start(bf16[8,4,80,1024]{3,2,1,0:T(8,128)(2,1)} %bitcast.131), calls=%async_computation.2 | async-start | bytes 10485760 | tf_op jit(solution)/shard_map/all_to_all | solution.py:90
  76.2 13.4 %scatter_custom_fusion = bf16[2560,1024]{1,0:T(8,128)(2,1)} fusion(s32[2048]{0:T(1024)S(1)} %bitcast.140, bf16[]{:T(256)} %constant.6.clone.1, bf16[256,1024]{1,0:T(8,128)(2,1)} %bitcast.134), kind=kCustom, calls=%fused_computation.19 | custom fusion | bytes 5767170 | tf_op jit(solution)/shard_map/scatter | solution.py:84
  89.6 100.5 %all-to-all-done.2 = bf16[8,4,80,1024]{3,2,1,0:T(8,128)(2,1)} async-done(((bf16[8,4,80,1024]{3,2,1,0:T(8,128)(2,1)}), bf16[8,4,80,1024]{3,2,1,0:T(8,128)(2,1)}, u32[]{:S(2)}, u32[]{:S(2)}) %all-to-all-start.2) | async-done | bytes 5242912 | tf_op jit(solution)/shard_map/all_to_all | solution.py:90
  190.0 5.7 %all-to-all-start = ((bf16[8,4,80,1024]{3,2,1,0:T(8,128)(2,1)}), bf16[8,4,80,1024]{3,2,1,0:T(8,128)(2,1)}, u32[]{:S(2)}, u32[]{:S(2)}) async-start(bf16[8,4,80,1024]{3,2,1,0:T(8,128)(2,1)} %bitcast.130), calls=%async_computation | async-start | bytes 10485760 | tf_op jit(solution)/shard_map/all_to_all | solution.py:89
  195.7 0.0 copy-done
  195.7 0.0 copy-start.3
  195.7 7.4 %fusion.5 = f32[4,8,80,384]{3,2,1,0:T(8,128)} fusion(bf16[8,4,80,1024]{3,2,1,0:T(8,128)(2,1)} %all-to-all-done.2, bf16[1,4,1024,384]{3,2,1,0:T(8,128)(2,1)S(1)} %copy-done), kind=kOutput, calls=%fused_computation.12 | convolution fusion | flops 2013265920 | bytes 12320768 | tf_op jit(solution)/shard_map/sepd,edf->sepf/dot_general | solution.py:14
  203.1 0.0 copy-done.3
  203.1 7.3 %fusion.7 = f32[4,8,80,384]{3,2,1,0:T(8,128)} fusion(bf16[8,4,80,1024]{3,2,1,0:T(8,128)(2,1)} %all-to-all-done.2, bf16[1,4,1024,384]{3,2,1,0:T(8,128)(2,1)S(1)} %copy-done.3), kind=kOutput, calls=%fused_computation.14 | convolution fusion | flops 2013265920 | bytes 12320768 | tf_op jit(solution)/shard_map/sepd,edf->sepf/dot_general | solution.py:15
  210.4 99.2 %all-to-all-done = bf16[8,4,80,1024]{3,2,1,0:T(8,128)(2,1)} async-done(((bf16[8,4,80,1024]{3,2,1,0:T(8,128)(2,1)}), bf16[8,4,80,1024]{3,2,1,0:T(8,128)(2,1)}, u32[]{:S(2)}, u32[]{:S(2)}) %all-to-all-start) | async-done | bytes 5242912 | tf_op jit(solution)/shard_map/all_to_all | solution.py:89
  309.6 0.0 copy-start.6
  309.6 10.9 %fusion.21 = (bf16[8,4,80]{2,0,1:T(8,128)(2,1)S(1)}, f32[4,8,80,384]{3,2,1,0:T(8,128)}) fusion(f32[4,8,80,384]{3,2,1,0:T(8,128)} %fusion.7, f32[4,8,80,384]{3,2,1,0:T(8,128)} %fusion.5, bf16[1,4,384,1024]{3,2,1,0:T(8,128)(2,1)} %param.17, bf16[8,4,80,1024]{3,2,1,0:T(8,128)(2,1)} %all-to-all-done), kind=kOutput, calls=%fused_computation.36 | convolution fusion | flops 2022110720 | bytes 20190208 | tf_op jit(solution)/shard_map/sepd,efd->sepf/dot_general | solution.py:19
  320.5 0.0 copy-done.6
  320.5 10.9 %fusion.22 = f32[4,8,80,1024]{3,2,1,0:T(8,128)} fusion(bf16[1,4,1024,384]{3,2,1,0:T(8,128)(2,1)S(1)} %copy-done, f32[4,8,80,384]{3,2,1,0:T(8,128)S(1)} %copy-done.6, f32[4,8,80,384]{3,2,1,0:T(8,128)} %fusion.7, f32[4,8,80,384]{3,2,1,0:T(8,128)} %get-tuple-element.29, f32[8,4,80]{2,0,1:T(8,128)S(1)} %copy_convert_fusion), kind=kOutput, calls=%fused_computation.38 | convolution fusion | flops 2024079360 | bytes 25438208 | tf_op jit(solution)/shard_map/sepf,edf->sepd/dot_general | solution.py:26
  331.3 13.0 %fusion = bf16[8,4,80,1024]{3,2,0,1:T(8,128)(2,1)} fusion(f32[4,8,80,1024]{3,2,1,0:T(8,128)} %fusion.22, bf16[1,4,1024,384]{3,2,1,0:T(8,128)(2,1)} %param.16, f32[4,8,80,384]{3,2,1,0:T(8,128)} %get-tuple-element.29, f32[8,4,80]{2,0,1:T(8,128)S(1)} %copy_convert_fusion, f32[4,8,80,384]{3,2,1,0:T(8,128)} %fusion.5), kind=kOutput, calls=%fused_computation.6 | convolution fusion | flops 2025390080 | bytes 26748928 | tf_op jit(solution)/shard_map/sepf,edf->sepd/dot_general | solution.py:27
  344.3 5.8 %copy.99 = bf16[8,4,80,1024]{3,2,1,0:T(8,128)(2,1)} copy(bf16[8,4,80,1024]{3,2,0,1:T(8,128)(2,1)} %fusion) | data formatting | bytes 10485760 | tf_op jit(solution)/shard_map/convert_element_type | solution.py:30
  350.1 0.0 copy-start.2
  350.1 0.0 copy-start.4
  350.1 5.8 %all-to-all-start.3 = ((bf16[8,4,80,1024]{3,2,1,0:T(8,128)(2,1)}), bf16[8,4,80,1024]{3,2,1,0:T(8,128)(2,1)}, u32[]{:S(2)}, u32[]{:S(2)}) async-start(bf16[8,4,80,1024]{3,2,1,0:T(8,128)(2,1)} %copy.99), calls=%async_computation.3 | async-start | bytes 10485760 | tf_op jit(solution)/shard_map/all_to_all | solution.py:95
  355.8 0.0 copy-done.2
  355.8 0.1 lt.45
  355.9 0.1 lt.46
  356.0 0.1 lt.42
  356.1 0.0 copy-done.4
  356.1 7.5 %convert_bitcast_fusion = bf16[1,4,1024,384]{3,2,1,0:T(8,128)(2,1)} fusion(bf16[1,4,640,1024]{3,2,1,0:T(8,128)(2,1)} %param.18, bf16[4,640]{1,0:T(4,128)(2,1)S(1)} %compare_convert_fusion, bf16[1,4,640,384]{3,2,1,0:T(8,128)(2,1)S(1)} %copy-done.4), kind=kOutput, calls=%fused_computation.44 | convolution fusion | flops 2017460224 | bytes 10359808 | tf_op jit(solution)/shard_map/esd,esf->edf/dot_general | solution.py:64
  363.6 0.6 copy.100
  364.2 105.6 %all-to-all-done.3 = bf16[8,4,80,1024]{3,2,1,0:T(8,128)(2,1)} async-done(((bf16[8,4,80,1024]{3,2,1,0:T(8,128)(2,1)}), bf16[8,4,80,1024]{3,2,1,0:T(8,128)(2,1)}, u32[]{:S(2)}, u32[]{:S(2)}) %all-to-all-start.3) | async-done | bytes 5242912 | tf_op jit(solution)/shard_map/all_to_all | solution.py:95
  469.8 5.6 %all-to-all-start.4 = ((bf16[8,4,80]{2,1,0:T(4,128)(2,1)}), bf16[8,4,80]{2,1,0:T(4,128)(2,1)S(1)}, u32[]{:S(2)}, u32[]{:S(2)}) async-start(bf16[8,4,80]{2,1,0:T(4,128)(2,1)} %copy.100), calls=%async_computation.4 | async-start | bytes 16384 | tf_op jit(solution)/shard_map/all_to_all | solution.py:96
  475.4 14.2 %gather_fusion = bf16[2048,1024]{1,0:T(8,128)(2,1)} fusion(bf16[2560,1024]{1,0:T(8,128)(2,1)} %bitcast.25, s32[2048]{0:T(1024)S(1)} %broadcast_clamp_fusion), kind=kCustom, calls=%fused_computation | custom fusion | bytes 8396800 | tf_op jit(solution)/shard_map/gather | solution.py:99
  489.5 0.0 copy-start.5
  489.5 6.4 %bitcast_reduce_fusion = bf16[256,1024]{1,0:T(8,128)(2,1)} fusion(bf16[2048,1024]{1,0:T(8,128)(2,1)} %gather_fusion), kind=kLoop, calls=%fused_computation.16 | loop fusion | flops 1835008 | bytes 4718592 | tf_op jit(solution)/shard_map/reduce_sum | solution.py:100
  496.0 3.2 collective-permute-start
  499.2 0.0 copy-done.5
  499.2 0.0 copy-start.1
  499.2 7.6 %convert_bitcast_fusion.1 = bf16[1,4,1024,384]{3,2,1,0:T(8,128)(2,1)} fusion(bf16[1,4,640,1024]{3,2,1,0:T(8,128)(2,1)} %param.18, bf16[4,640]{1,0:T(4,128)(2,1)S(1)} %compare_convert_fusion, bf16[1,4,640,384]{3,2,1,0:T(8,128)(2,1)S(1)} %copy-done.5), kind=kOutput, calls=%fused_computation.45 | convolution fusion | flops 2017460224 | bytes 10359808 | tf_op jit(solution)/shard_map/esd,esf->edf/dot_general | solution.py:61
  506.9 0.0 all-to-all-done.4
  506.9 0.1 reshape.111
  506.9 13.1 %gather_fusion.1 = bf16[2048]{0:T(1024)(128)(2,1)S(1)} fusion(bf16[2560]{0:T(1024)(128)(2,1)S(1)} %reshape.111, s32[2048]{0:T(1024)S(1)} %broadcast_clamp_fusion), kind=kCustom, calls=%fused_computation.1 | custom fusion | bytes 16384 | tf_op jit(solution)/shard_map/gather | solution.py:101
  520.0 0.1 broadcast_in_dim_reshape.3
  520.1 0.7 copy.103
  520.8 0.0 collective-permute-done
  520.8 1.9 copy.122
  522.7 0.0 copy-done.1
  (5 shorter events, 0.0 us)
Async XLA Ops:
  0.6 195.0 %copy-start = (bf16[1,4,1024,384]{3,2,1,0:T(8,128)(2,1)S(1)}, bf16[1,4,1024,384]{3,2,1,0:T(8,128)(2,1)}, u32[]{:S(2)}) copy-start(bf16[1,4,1024,384]{3,2,1,0:T(8,128)(2,1)} %param.15) | copy-start | bytes 9437188
  39.8 19.1 %all-to-all-start.1 = ((bf16[8,4,80]{2,1,0:T(4,128)(2,1)}), bf16[8,4,80]{2,1,0:T(4,128)(2,1)S(1)}, u32[]{:S(2)}, u32[]{:S(2)}) async-start(bf16[8,4,80]{2,1,0:T(4,128)(2,1)} %reshape.106), calls=%async_computation.1 | async-start | bytes 16384 | tf_op jit(solution)/shard_map/all_to_all | solution.py:91
  58.9 131.2 %all-to-all-start.2 = ((bf16[8,4,80,1024]{3,2,1,0:T(8,128)(2,1)}), bf16[8,4,80,1024]{3,2,1,0:T(8,128)(2,1)}, u32[]{:S(2)}, u32[]{:S(2)}) async-start(bf16[8,4,80,1024]{3,2,1,0:T(8,128)(2,1)} %bitcast.131), calls=%async_computation.2 | async-start | bytes 10485760 | tf_op jit(solution)/shard_map/all_to_all | solution.py:90
  190.0 119.6 %all-to-all-start = ((bf16[8,4,80,1024]{3,2,1,0:T(8,128)(2,1)}), bf16[8,4,80,1024]{3,2,1,0:T(8,128)(2,1)}, u32[]{:S(2)}, u32[]{:S(2)}) async-start(bf16[8,4,80,1024]{3,2,1,0:T(8,128)(2,1)} %bitcast.130), calls=%async_computation | async-start | bytes 10485760 | tf_op jit(solution)/shard_map/all_to_all | solution.py:89
  195.7 7.4 %copy-start.3 = (bf16[1,4,1024,384]{3,2,1,0:T(8,128)(2,1)S(1)}, bf16[1,4,1024,384]{3,2,1,0:T(8,128)(2,1)}, u32[]{:S(2)}) copy-start(bf16[1,4,1024,384]{3,2,1,0:T(8,128)(2,1)} %param.16) | copy-start | bytes 9437188
  309.6 10.9 %copy-start.6 = (f32[4,8,80,384]{3,2,1,0:T(8,128)S(1)}, f32[4,8,80,384]{3,2,1,0:T(8,128)}, u32[]{:S(2)}) copy-start(f32[4,8,80,384]{3,2,1,0:T(8,128)} %fusion.5) | copy-start | bytes 11796484
  350.1 5.8 %copy-start.2 = (s32[1,4,8]{2,1,0:T(4,128)S(1)}, s32[1,4,8]{2,1,0:T(4,128)}, u32[]{:S(2)}) copy-start(s32[1,4,8]{2,1,0:T(4,128)} %param.21) | copy-start | bytes 388
  350.1 6.0 %copy-start.4 = (bf16[1,4,640,384]{3,2,1,0:T(8,128)(2,1)S(1)}, bf16[1,4,640,384]{3,2,1,0:T(8,128)(2,1)}, u32[]{:S(2)}) copy-start(bf16[1,4,640,384]{3,2,1,0:T(8,128)(2,1)} %param.20) | copy-start | bytes 5898244
  350.1 119.7 %all-to-all-start.3 = ((bf16[8,4,80,1024]{3,2,1,0:T(8,128)(2,1)}), bf16[8,4,80,1024]{3,2,1,0:T(8,128)(2,1)}, u32[]{:S(2)}, u32[]{:S(2)}) async-start(bf16[8,4,80,1024]{3,2,1,0:T(8,128)(2,1)} %copy.99), calls=%async_computation.3 | async-start | bytes 10485760 | tf_op jit(solution)/shard_map/all_to_all | solution.py:95
  469.8 37.1 %all-to-all-start.4 = ((bf16[8,4,80]{2,1,0:T(4,128)(2,1)}), bf16[8,4,80]{2,1,0:T(4,128)(2,1)S(1)}, u32[]{:S(2)}, u32[]{:S(2)}) async-start(bf16[8,4,80]{2,1,0:T(4,128)(2,1)} %copy.100), calls=%async_computation.4 | async-start | bytes 16384 | tf_op jit(solution)/shard_map/all_to_all | solution.py:96
  489.5 9.7 %copy-start.5 = (bf16[1,4,640,384]{3,2,1,0:T(8,128)(2,1)S(1)}, bf16[1,4,640,384]{3,2,1,0:T(8,128)(2,1)}, u32[]{:S(2)}) copy-start(bf16[1,4,640,384]{3,2,1,0:T(8,128)(2,1)} %param.19) | copy-start | bytes 5898244
  496.0 24.9 %collective-permute-start = (bf16[1,256,1024]{2,1,0:T(8,128)(2,1)}, bf16[1,256,1024]{2,1,0:T(8,128)(2,1)}, u32[]{:S(2)}, u32[]{:S(2)}) collective-permute-start(bf16[1,256,1024]{2,1,0:T(8,128)(2,1)} %bitcast.27), channel_id=1, source_target_pairs={{8,0},{16,8},{24,16},{9,1},{17,9},{25,17},{10,2},{18,10},{26,18},{... | collective-permute-start | bytes 1572872 | tf_op jit(solution)/shard_map/ppermute | solution.py:10
  499.2 23.5 %copy-start.1 = (bf16[1,4,1024,384]{3,2,1,0:T(8,128)(2,1)S(1)}, bf16[1,4,1024,384]{3,2,1,0:T(8,128)(2,1)}, u32[]{:S(2)}) copy-start(bf16[1,4,1024,384]{3,2,1,0:T(8,128)(2,1)} %param.15) | copy-start | bytes 9437188
where the time goes:
time: 527 us; the launch traced here: 523 us
  waiting for transfers between devices  305 us (58%)
  local copies, waits for them, and re-layouts  83 us (16%)
  matrix products  64.5 us (12%)
  starting transfers between devices  43.3 us (8%)
  other arithmetic  25.9 us (5%)
    all_to_all x1, waiting for transfers between devices, per_device(): lax.all_to_all(slot_grad, 'ep', split_axis=0, concat_axis=0, tiled=True)  106 us
    all_to_all x1, waiting for transfers between devices, per_device(): lax.all_to_all(send_input, 'ep', split_axis=0, concat_axis=0, tiled=True)  100 us
    all_to_all x1, waiting for transfers between devices, per_device(): lax.all_to_all(send_grad, 'ep', split_axis=0, concat_axis=0, tiled=True)  99.2 us
    scatter x2, local copies, waits for them, and re-layouts, per_device(): jnp.zeros((experts_all * capacity, width), jnp.bfloat16).at[place]  26.7 us
    all_to_all x1, starting transfers between devices, per_device(): lax.all_to_all(send_input, 'ep', split_axis=0, concat_axis=0, tiled=True)  17.3 us
    another operation x3, other arithmetic  16.9 us
    scatter x1, local copies, waits for them, and re-layouts, per_device(): jnp.zeros((experts_all * capacity,), jnp.bfloat16).at[place]  14.6 us
    gather x1, local copies, waits for them, and re-layouts, per_device(): back_grad[place].reshape(tok_rows, top_count, width).astype(jnp.float32)  14.2 us
  transfers between devices with their start and end apart: 6, of which 3 were waited for; matrix products, arithmetic and copies ran while one was open for 18% of the time, Pallas kernels for 0%

commit v1 on v0

v1 whole, which is shorter than its diff:
```python
import jax
import jax.numpy as jnp
from jax import lax
from jax.sharding import PartitionSpec as P

F32 = jnp.float32
BF16 = jnp.bfloat16


def from_behind(array, axis, by):
    devices = lax.axis_size(axis)
    pairs = [(i, i + by) for i in range(devices) if 0 <= i + by < devices]
    return lax.ppermute(array, axis, pairs)


def per_device(
    output_grad,
    layer_input,
    expert_ids,
    route_probs,
    gate_weight,
    up_weight,
    down_weight,
    saved_inputs,
    saved_gate_grad,
    saved_up_grad,
    saved_counts,
):
    ep_count = lax.axis_size("ep")
    me = lax.axis_index("ep")
    w_gate = gate_weight[0]
    w_up = up_weight[0]
    w_down = down_weight[0]
    local_experts = w_gate.shape[0]
    experts_all = local_experts * ep_count
    slots_all = saved_inputs.shape[2]
    capacity = slots_all // ep_count
    tok_rows = expert_ids.shape[1]
    top_count = expert_ids.shape[2]
    width = output_grad.shape[2]

    small = jnp.concatenate([expert_ids[0].astype(BF16), route_probs[0]], axis=1)
    small = jnp.pad(small, ((0, 0), (0, 128 - small.shape[1])))
    packed = jnp.concatenate([output_grad[0], layer_input[0], small], axis=1)
    everyone = lax.all_gather(packed, "ep", axis=0, tiled=False)

    live = jnp.arange(capacity, dtype=jnp.int32)[None, None, :] < saved_counts[0][:, :, None]
    masked = saved_inputs[0] * live.reshape(local_experts, slots_all).astype(BF16)[:, :, None]
    gate_part = jnp.einsum(
        "esd,esf->edf", masked, saved_gate_grad[0], preferred_element_type=F32
    ).astype(BF16)
    up_part = jnp.einsum(
        "esd,esf->edf", masked, saved_up_grad[0], preferred_element_type=F32
    ).astype(BF16)

    ids_all = everyone[:, :, 2 * width : 2 * width + top_count].astype(jnp.int32)
    probs_all = everyone[:, :, 2 * width + top_count : 2 * width + 2 * top_count].astype(F32)
    mine = me * local_experts + jnp.arange(local_experts, dtype=jnp.int32)
    hit = ids_all[:, None, :, :] == mine[None, :, None, None]
    member = jnp.any(hit, axis=3)
    prob = jnp.sum(jnp.where(hit, probs_all[:, None], 0.0), axis=3)
    lower = jnp.tril(jnp.ones((tok_rows, tok_rows), BF16), -1)
    before = jnp.einsum("sen,tn->set", member.astype(BF16), lower, preferred_element_type=F32)
    slot = jnp.where(member, before.astype(jnp.int32), -1)
    chosen = slot[:, :, None, :] == jnp.arange(capacity, dtype=jnp.int32)[None, None, :, None]
    pick = chosen.astype(BF16)
    put = jnp.where(chosen, prob[:, :, None, :], 0.0).astype(BF16)
    rows = jnp.einsum(
        "sect,std->escd", pick, everyone[:, :, : 2 * width], preferred_element_type=F32
    ).astype(BF16)
    rows = rows.reshape(local_experts, slots_all, 2 * width)
    grad_part = rows[:, :, :width]
    input_part = rows[:, :, width:]

    gate_pre = jnp.einsum("epd,edf->epf", input_part, w_gate, preferred_element_type=F32)
    up_pre = jnp.einsum("epd,edf->epf", input_part, w_up, preferred_element_type=F32)
    sigma = jax.nn.sigmoid(gate_pre)
    active = gate_pre * sigma
    hidden = active * up_pre
    hidden_grad = jnp.einsum("epd,efd->epf", grad_part, w_down, preferred_element_type=F32)
    slot_prob = jnp.sum(hidden_grad * hidden, axis=2).astype(BF16)
    gate_grad = (hidden_grad * up_pre * sigma * (1.0 + gate_pre * (1.0 - sigma))).astype(BF16)
    up_grad = (hidden_grad * active).astype(BF16)
    slot_grad = jnp.einsum("epf,edf->epd", gate_grad, w_gate, preferred_element_type=F32)
    slot_grad = slot_grad + jnp.einsum("epf,edf->epd", up_grad, w_up, preferred_element_type=F32)
    slot_grad = slot_grad.astype(BF16).reshape(local_experts, ep_count, capacity, width)
    token_grad = jnp.einsum("sect,escd->std", put, slot_grad, preferred_element_type=F32)
    slot_prob = slot_prob.reshape(local_experts, ep_count, capacity)
    token_prob = jnp.einsum("sect,esc->ste", pick, slot_prob, preferred_element_type=F32)
    spread = jnp.where(
        (jnp.arange(ep_count) == me)[None, None, :, None], token_prob[:, :, None, :], 0.0
    ).reshape(ep_count, tok_rows, experts_all)
    pad = -experts_all % 128
    back = jnp.concatenate([token_grad, jnp.pad(spread, ((0, 0), (0, 0), (0, pad)))], axis=2)
    summed = lax.psum_scatter(back.astype(BF16), "ep", scatter_dimension=0, tiled=False)
    input_grad = summed[:, :width]
    own = expert_ids[0][:, :, None] == jnp.arange(experts_all, dtype=jnp.int32)[None, None, :]
    prob_part = jnp.sum(
        jnp.where(own, summed[:, None, width : width + experts_all].astype(F32), 0.0), axis=2
    ).astype(BF16)
    upstream = from_behind(input_grad[None], "section", -1)
    return (upstream, prob_part[None], gate_part[None], up_part[None])


def solution(mesh):
    three = P("section", "ep", None)
    four = P("section", "ep", None, None)
    return jax.shard_map(
        per_device,
        mesh=mesh,
        in_specs=(three, three, three, three, four, four, four, four, four, four, three),
        out_specs=(three, three, four, four),
        check_vma=False,
    )
```

time: 527 us -> 336 us (0.64)
  waiting for transfers between devices: 305 us -> 217 us
  local copies, waits for them, and re-layouts: 83 us -> 18.9 us
  starting transfers between devices: 43.3 us -> 3.04 us
  other arithmetic: 25.9 us -> 8.01 us
  between operations: 1.24 us -> 14.2 us
  matrix products: 64.5 us -> 74.3 us
    all_to_all x5 -> x0, waiting for transfers between devices: 305 us -> none  [the longest x1 106 us: per_device(): lax.all_to_all(slot_grad, 'ep', split_axis=0, concat_axis=0, tiled=True)]
    all_gather x0 -> x1, waiting for transfers between devices: none -> 129 us  [per_device(): everyone = lax.all_gather(packed, 'ep', axis=0, tiled=False)]
    reduce_scatter x0 -> x1, waiting for transfers between devices: none -> 87.3 us  [per_device(): lax.psum_scatter(back.astype(BF16), 'ep', scatter_dimension=0, tiled=False)]
    scatter x3 -> x0, local copies, waits for them, and re-layouts: 41.3 us -> none  [the longest x2 26.7 us: per_device(): jnp.zeros((experts_all * capacity, width), jnp.bfloat16).at[place]]
    all_to_all x5 -> x0, starting transfers between devices: 40 us -> none  [the longest x1 17.3 us: per_device(): lax.all_to_all(send_input, 'ep', split_axis=0, concat_axis=0, tiled=True)]
    gather x2 -> x0, local copies, waits for them, and re-layouts: 27.2 us -> none  [the longest x1 14.2 us: per_device(): back_grad[place].reshape(tok_rows, top_count, width).astype(jnp.float32)]
    another operation x3 -> x1, other arithmetic: 16.9 us -> 0.09 us
    dot_general x5 -> x9, matrix products: 49.4 us -> 58.6 us  [the longest x1 13 us: per_device(): jnp.einsum('epf,edf->epd', up_grad, w_up, preferred_element_type=F32)]
  transfers between devices with their start and end apart: 6 -> 3, of which waited for: 3 -> 2; matrix products, arithmetic and copies ran while one was open for 18% -> 5% of each run, Pallas kernels for 0% -> 0%
where the time goes in v1:
time: 336 us; the launch traced here: 335 us
  waiting for transfers between devices  217 us (65%)
  matrix products  74.3 us (22%)
  local copies, waits for them, and re-layouts  18.9 us (6%)
  between operations  14.2 us (4%)
  other arithmetic  8.01 us (2%)
    all_gather x1, waiting for transfers between devices, per_device(): everyone = lax.all_gather(packed, 'ep', axis=0, tiled=False)  129 us
    reduce_scatter x1, waiting for transfers between devices, per_device(): lax.psum_scatter(back.astype(BF16), 'ep', scatter_dimension=0, tiled=False)  87.3 us
    dot_general x1, matrix products, per_device(): jnp.einsum('epf,edf->epd', up_grad, w_up, preferred_element_type=F32)  13 us
    dot_general x1, matrix products, per_device(): jnp.einsum('epf,edf->epd', gate_grad, w_gate, preferred_element_type=F32)  12.2 us
    convert_element_type x1, local copies, waits for them, and re-layouts, per_device(): rows = jnp.einsum('sect,std->escd', pick, everyone[:, :, :2 * width], pre...  10 us
    dot_general x1, matrix products, per_device(): jnp.einsum('sect,std->escd', pick, everyone[:, :, :2 * width], preferred_...  8.85 us
    dot_general x1, matrix products, per_device(): jnp.einsum('esd,esf->edf', masked, saved_gate_grad[0], preferred_element_...  8.21 us
    dot_general x1, matrix products, per_device(): jnp.einsum('esd,esf->edf', masked, saved_up_grad[0], preferred_element_ty...  7.48 us
  transfers between devices with their start and end apart: 3, of which 2 were waited for; matrix products, arithmetic and copies ran while one was open for 5% of the time, Pallas kernels for 0%

profile of v1, /device:TPU:9, one launch (start us, length us, event | category | flops | bytes accessed | tf_op | source)
XLA Modules:
  0.0 335.1 jit_solution(8158631794143276215)
XLA Ops:
  7.2 0.0 copy-start
  7.2 0.0 all-gather.3.cloned.1.call-start
  7.2 0.9 bitcast_convert_fusion.1
  8.1 0.7 pad_maximum_fusion
  8.8 0.1 copy.88
  8.9 2.3 fusion.34
  11.2 0.0 all-gather.3.cloned.1.call-update
  11.2 0.0 reduce-scatter.2.cloned.1.call-start
  11.3 0.1 broadcast_in_dim.102
  11.4 0.1 broadcast_in_dim.103
  11.5 129.3 %all-gather.3.cloned.1.call-done = bf16[2048,2176]{1,0:T(8,128)(2,1)} async-done(((bf16[256,2176]{1,0:T(8,128)(2,1)}), bf16[2048,2176]{1,0:T(8,128)(2,1)}) %all-gather.3.cloned.1.call-update) | async-done | bytes 8912912 | tf_op jit(solution)/shard_map/all_gather | solution.py:45
  140.8 2.5 fusion.52
  143.3 1.2 copy.116
  144.5 0.2 compare_reduce_fusion
  144.7 0.2 fusion.35
  145.0 8.8 %convert_bitcast_fusion = bf16[4,8,80,2048]{3,2,0,1:T(8,128)(2,1)} fusion(bf16[8,256,2176]{2,1,0:T(8,128)(2,1)} %bitcast.77, s32[8,4,256]{2,1,0:T(4,128)S(1)} %copy.92), kind=kOutput, calls=%fused_computation.1 | convolution fusion | flops 2690252800 | bytes 18907136 | tf_op jit(solution)/shard_map/sect,std->escd/dot_general | solution.py:68
  153.8 10.0 %copy.94 = bf16[4,8,80,2048]{3,2,1,0:T(8,128)(2,1)} copy(bf16[4,8,80,2048]{3,2,0,1:T(8,128)(2,1)} %convert_bitcast_fusion) | data formatting | bytes 20971520 | tf_op jit(solution)/shard_map/convert_element_type | solution.py:70
  163.8 0.0 copy-done
  163.8 0.0 copy-start.2
  163.8 0.0 copy-start.7
  163.8 7.2 %fusion.9 = f32[4,640,384]{1,2,0:T(8,128)} fusion(bf16[4,640,2048]{2,1,0:T(8,128)(2,1)} %bitcast.68, bf16[1,4,1024,384]{3,2,1,0:T(8,128)(2,1)S(1)} %copy-done), kind=kOutput, calls=%fused_computation.15 | convolution fusion | flops 2013265920 | bytes 12320768 | tf_op jit(solution)/shard_map/epd,edf->epf/dot_general | solution.py:75
  171.0 0.0 copy-done.2
  171.0 0.0 copy-done.7
  171.0 0.0 copy-start.6
  171.0 4.8 %fusion.11 = f32[4,640,384]{1,2,0:T(8,128)} fusion(bf16[4,640,2048]{2,1,0:T(8,128)(2,1)S(1)} %bitcast.69, bf16[1,4,1024,384]{3,2,1,0:T(8,128)(2,1)S(1)} %copy-done.7), kind=kOutput, calls=%fused_computation.17 | convolution fusion | flops 2013265920 | bytes 12320768 | tf_op jit(solution)/shard_map/epd,edf->epf/dot_general | solution.py:76
  175.8 0.0 copy-done.6
  175.8 6.7 %multiply_reduce_fusion = (bf16[4,640]{1,0:T(4,128)(2,1)S(1)}, f32[4,640,384]{1,2,0:T(8,128)}) fusion(f32[4,640,384]{1,2,0:T(8,128)} %fusion.11, f32[4,640,384]{1,2,0:T(8,128)} %fusion.9, bf16[1,4,384,1024]{3,2,1,0:T(8,128)(2,1)S(1)} %copy-done.6, bf16[4,640,2048]{2,1,0:T(8,128)(2,1)S(1)} %bitcast.70), kind=kOutput, calls=%fused_computation.19 | convolution fusion | flops 2020144640 | bytes 20190208 | tf_op jit(solution)/shard_map/epd,efd->epf/dot_general | solution.py:80
  182.5 12.2 %fusion.14 = f32[4,640,1024]{2,1,0:T(8,128)} fusion(bf16[1,4,1024,384]{3,2,1,0:T(8,128)(2,1)S(1)} %copy-done, f32[4,640,384]{1,2,0:T(8,128)} %fusion.9, f32[4,640,384]{1,2,0:T(8,128)} %get-tuple-element.19, f32[4,640,384]{1,2,0:T(8,128)} %fusion.11), kind=kOutput, calls=%fused_computation.24 | convolution fusion | flops 2023096320 | bytes 25427968 | tf_op jit(solution)/shard_map/epf,edf->epd/dot_general | solution.py:84
  194.7 0.0 copy-start.3
  194.7 13.0 %add_convert_fusion = bf16[4,640,1024]{2,1,0:T(8,128)(2,1)} fusion(f32[4,640,1024]{2,1,0:T(8,128)} %fusion.14, bf16[1,4,1024,384]{3,2,1,0:T(8,128)(2,1)} %param.16, f32[4,640,384]{1,2,0:T(8,128)} %get-tuple-element.19, f32[4,640,384]{1,2,0:T(8,128)} %fusion.9), kind=kOutput, calls=%fused_computation | convolution fusion | flops 2024407040 | bytes 26738688 | tf_op jit(solution)/shard_map/epf,edf->epd/dot_general | solution.py:85
  207.7 0.0 copy-done.3
  207.7 0.2 copy.117
  207.9 0.2 fusion.37
  208.1 0.1 reshape.73
  208.2 0.5 fusion.24
  208.7 5.1 %bitcast_convert_fusion = bf16[8,256,1024]{1,2,0:T(8,128)(2,1)S(1)} fusion(bf16[4,8,80,1024]{3,2,1,0:T(8,128)(2,1)} %bitcast.83, bf16[8,4,256]{2,1,0:T(4,128)(2,1)S(1)} %fusion.37, s32[8,4,256]{2,1,0:T(4,128)S(1)} %copy.92), kind=kOutput, calls=%fused_computation.6 | convolution fusion | flops 1345585152 | bytes 9486336 | tf_op jit(solution)/shard_map/sect,escd->std/dot_general | solution.py:87
  213.8 0.1 fusion.38
  213.9 2.3 fusion.6
  216.2 0.0 copy-start.5
  216.2 0.0 copy-start.8
  216.3 0.0 reduce-scatter.2.cloned.1.call-update
  216.3 0.7 copy-done.5
  216.9 0.1 lt.30
  217.0 0.1 lt.31
  217.1 0.1 lt.27
  217.2 0.6 copy-done.8
  217.8 7.5 %convert_bitcast_fusion.1 = bf16[1,4,1024,384]{3,2,1,0:T(8,128)(2,1)} fusion(bf16[1,4,640,1024]{3,2,1,0:T(8,128)(2,1)} %param.18, bf16[4,640]{1,0:T(4,128)(2,1)S(1)} %compare_convert_fusion, bf16[1,4,640,384]{3,2,1,0:T(8,128)(2,1)S(1)} %copy-done.8), kind=kOutput, calls=%fused_computation.30 | convolution fusion | flops 2017460224 | bytes 10359808 | tf_op jit(solution)/shard_map/esd,esf->edf/dot_general | solution.py:52
  225.3 87.3 %reduce-scatter.2.cloned.1.call-done = bf16[1,256,1152]{1,2,0:T(8,128)(2,1)} async-done(((bf16[8,256,1152]{1,2,0:T(8,128)(2,1)}), bf16[1,256,1152]{1,2,0:T(8,128)(2,1)}) %reduce-scatter.2.cloned.1.call-update) | async-done | bytes 589840 | tf_op jit(solution)/shard_map/reduce_scatter | solution.py:95
  312.6 1.1 slice_bitcast_fusion.4
  313.7 0.0 copy-start.4
  313.7 3.0 collective-permute-start
  316.6 0.0 copy-start.1
  316.6 8.2 %convert_bitcast_fusion.2 = bf16[1,4,1024,384]{3,2,1,0:T(8,128)(2,1)} fusion(bf16[1,4,640,1024]{3,2,1,0:T(8,128)(2,1)} %param.18, bf16[4,640]{1,0:T(4,128)(2,1)S(1)} %compare_convert_fusion, bf16[1,4,640,384]{3,2,1,0:T(8,128)(2,1)} %param.19), kind=kOutput, calls=%fused_computation.31 | convolution fusion | flops 2017460224 | bytes 10359808 | tf_op jit(solution)/shard_map/esd,esf->edf/dot_general | solution.py:49
  324.8 0.7 slice_convert_fusion
  325.6 0.0 copy-done.4
  325.6 0.6 select_reduce_fusion
  326.2 0.0 collective-permute-done
  326.2 2.0 copy.104
  328.3 0.0 copy-done.1
  (10 shorter events, 0.1 us)
Async XLA Ops:
  7.2 156.7 %copy-start = (bf16[1,4,1024,384]{3,2,1,0:T(8,128)(2,1)S(1)}, bf16[1,4,1024,384]{3,2,1,0:T(8,128)(2,1)}, u32[]{:S(2)}) copy-start(bf16[1,4,1024,384]{3,2,1,0:T(8,128)(2,1)} %param.15) | copy-start | bytes 9437188
  7.2 133.7 %all-gather.3.cloned.1.call-start = ((), (), s32[]{:S(2)}) async-start(), calls=%async_computation.2 | async-start | bytes 10027008 | tf_op jit(solution)/shard_map/all_gather | solution.py:45
  11.2 301.3 %reduce-scatter.2.cloned.1.call-start = ((), (), s32[]{:S(2)}) async-start(), calls=%async_computation.1 | async-start | bytes 5308416 | tf_op jit(solution)/shard_map/reduce_scatter | solution.py:95
  163.8 7.2 %copy-start.2 = (bf16[4,8,80,2048]{3,2,1,0:T(8,128)(2,1)S(1)}, bf16[4,8,80,2048]{3,2,1,0:T(8,128)(2,1)}, u32[]{:S(2)}) copy-start(bf16[4,8,80,2048]{3,2,1,0:T(8,128)(2,1)} %copy.94) | copy-start | bytes 31457284
  163.8 7.2 %copy-start.7 = (bf16[1,4,1024,384]{3,2,1,0:T(8,128)(2,1)S(1)}, bf16[1,4,1024,384]{3,2,1,0:T(8,128)(2,1)}, u32[]{:S(2)}) copy-start(bf16[1,4,1024,384]{3,2,1,0:T(8,128)(2,1)} %param.16) | copy-start | bytes 9437188
  171.0 4.8 %copy-start.6 = (bf16[1,4,384,1024]{3,2,1,0:T(8,128)(2,1)S(1)}, bf16[1,4,384,1024]{3,2,1,0:T(8,128)(2,1)}, u32[]{:S(2)}) copy-start(bf16[1,4,384,1024]{3,2,1,0:T(8,128)(2,1)} %param.17) | copy-start | bytes 9437188
  194.7 13.0 %copy-start.3 = (bf16[8,256,8]{2,1,0:T(8,128)(2,1)S(1)}, bf16[8,256,8]{2,1,0:T(8,128)(2,1)}, u32[]{:S(2)}) copy-start(bf16[8,256,8]{2,1,0:T(8,128)(2,1)} %get-tuple-element.16) | copy-start | bytes 98308
  216.2 0.7 copy-start.5
  216.2 1.6 copy-start.8
  313.7 11.9 %copy-start.4 = (s32[1,256,8]{1,2,0:T(8,128)S(1)}, s32[1,256,8]{1,2,0:T(8,128)}, u32[]{:S(2)}) copy-start(s32[1,256,8]{1,2,0:T(8,128)} %param.13) | copy-start | bytes 24580
  313.7 12.6 %collective-permute-start = (bf16[1,256,1024]{1,2,0:T(8,128)(2,1)S(1)}, bf16[1,256,1024]{1,2,0:T(8,128)(2,1)}, u32[]{:S(2)}, u32[]{:S(2)}) collective-permute-start(bf16[1,256,1024]{1,2,0:T(8,128)(2,1)S(1)} %slice_bitcast_fusion.4), channel_id=1, source_target_pairs={{8,0},{16,8},{24,16},{9,1},{17,9},{25,17},{10,2},{18,10},{26,18},{... | collective-permute-start | bytes 1572872 | tf_op jit(solution)/shard_map/ppermute | solution.py:13
  316.6 11.6 %copy-start.1 = (bf16[1,4,1024,384]{3,2,1,0:T(8,128)(2,1)S(1)}, bf16[1,4,1024,384]{3,2,1,0:T(8,128)(2,1)}, u32[]{:S(2)}) copy-start(bf16[1,4,1024,384]{3,2,1,0:T(8,128)(2,1)} %param.15) | copy-start | bytes 9437188
Sparse Core Ops, SparseCore 0:
  11.4 129.4 all-gather.2
  216.4 96.1 reduce-scatter.1

commit v2 on v1

v2 whole, which is shorter than its diff:
```python
import functools

import jax
import jax.numpy as jnp
from jax import lax
from jax.experimental import pallas as pl
from jax.experimental.pallas import tpu as pltpu
from jax.sharding import PartitionSpec as P

F32 = jnp.float32
BF16 = jnp.bfloat16
MESH = pl.DeviceIdType.MESH
VMEM = pl.BlockSpec(memory_space=pltpu.VMEM)
ANY = pl.BlockSpec(memory_space=pl.ANY)


class Copies:
    def __init__(self, send, recv):
        self.send, self.recv, self.used, self.items = send, recv, 0, []

    def make(self, src, dst, target):
        at = self.used
        self.used += 1
        copy = pltpu.make_async_remote_copy(
            src_ref=src,
            dst_ref=dst,
            send_sem=self.send.at[at],
            recv_sem=self.recv.at[at],
            device_id=target,
            device_id_type=MESH,
        )
        self.items.append(copy)
        return copy

    def start(self, src, dst, target):
        copy = self.make(src, dst, target)
        copy.start()
        return copy


def place_of(count):
    me = lax.axis_index("ep")
    outer, inner = me // 2, me % 2
    ring = count // 2
    up = ((outer + 1) % ring) * 2 + inner
    down = ((outer + ring - 1) % ring) * 2 + inner
    return me, outer, inner, ring, (up, down), outer * 2 + 1 - inner


def gather_copies(count):
    ring = count // 2
    return 6 * (ring - 1) + 2 * (ring - 1) + 2 + (count - 1)


def gather_kernel(count, g, x, s, g_all, x_all, s_all, local, send, recv):
    me, outer, inner, ring, sides, partner = place_of(count)
    tokens = g.shape[0]
    half = tokens // 2
    rows = (pl.ds(0, half), pl.ds(half, half))
    copies = Copies(send, recv)
    own = [
        pltpu.make_async_copy(g, g_all.at[me], local.at[0]),
        pltpu.make_async_copy(x, x_all.at[me], local.at[1]),
        pltpu.make_async_copy(s, s_all.at[me], local.at[2]),
    ]
    for copy in own:
        copy.start()
    barrier = pltpu.get_barrier_semaphore()
    for away in range(1, count):
        pl.semaphore_signal(
            barrier, inc=1, device_id={"ep": (me + away) % count}, device_id_type=MESH
        )
    pl.semaphore_wait(barrier, count - 1)

    def block(step, side, row):
        return ((outer + (-step if side == 0 else step) + ring) % ring) * 2 + row

    def hop(ref, all_ref, step, side, row):
        at = block(step, side, row)
        dst = all_ref.at[at, rows[side]]
        source = dst if ref is None else ref.at[rows[side]]
        return copies.start(source, dst, {"ep": sides[side]})

    side_list = (0, 1)
    other = 1 - inner
    x_now = [hop(x, x_all, 0, side, inner) for side in side_list]
    g_across = copies.start(g, g_all.at[me], {"ep": partner})
    g_now = [hop(g, g_all, 0, side, inner) for side in side_list]
    x_across = copies.start(x, x_all.at[me], {"ep": partner})
    tiny = [
        copies.start(s, s_all.at[me], {"ep": (me + away) % count}) for away in range(1, count)
    ]
    g_other = None
    late = [x_across] + tiny
    for step in range(ring - 1):
        more = step < ring - 2
        x_next = []
        for side in side_list:
            x_now[side].wait_recv()
            if more:
                x_next.append(hop(None, x_all, step + 1, side, inner))
            got = x_all.at[block(step + 1, side, inner), rows[side]]
            late.append(copies.start(got, got, {"ep": partner}))
        x_now = x_next
        g_next = []
        for side in side_list:
            g_now[side].wait_recv()
            if more:
                g_next.append(hop(None, g_all, step + 1, side, inner))
        g_now = g_next
        if step == 0:
            g_across.wait_recv()
        else:
            for copy in g_other:
                copy.wait_recv()
        g_other = [hop(None, g_all, step, side, other) for side in side_list]
    for copy in g_other + late:
        copy.wait_recv()
    for copy in copies.items:
        copy.wait_send()
    for copy in own:
        copy.wait()


def gather_tokens(count, g, x, s):
    pairs = gather_copies(count)
    return pl.pallas_call(
        functools.partial(gather_kernel, count),
        out_shape=[jax.ShapeDtypeStruct((count,) + a.shape, a.dtype) for a in (g, x, s)],
        in_specs=[VMEM] * 3,
        out_specs=[ANY] * 3,
        scratch_shapes=[
            pltpu.SemaphoreType.DMA((3,)),
            pltpu.SemaphoreType.DMA((pairs,)),
            pltpu.SemaphoreType.DMA((pairs,)),
        ],
        compiler_params=pltpu.CompilerParams(collective_id=0, has_side_effects=True),
    )(g, x, s)


def scatter_copies(count):
    ring = count // 2
    return 6 * (ring - 1) + ring + 2 + (count - 1)


def add(a, b):
    return (a.astype(F32) + b.astype(F32)).astype(BF16)


def scatter_kernel(
    count, sections, part, prob, out, prob_out, a_ring, b_ring, b_across, a_take, land,
    total, send, recv, shift_send, shift_recv,
):
    me, outer, inner, ring, sides, partner = place_of(count)
    section = lax.axis_index("section")
    tokens, width = out.shape
    half, wide = tokens // 2, width // 2
    rows = (pl.ds(0, half), pl.ds(half, half))
    left, right = pl.ds(0, wide), pl.ds(wide, wide)
    copies = Copies(send, recv)
    barrier = pltpu.get_barrier_semaphore()
    for away in range(1, count):
        pl.semaphore_signal(
            barrier, inc=1, device_id={"ep": (me + away) % count}, device_id_type=MESH
        )
    for away in (1, sections - 1):
        pl.semaphore_signal(
            barrier, inc=1, device_id={"section": (section + away) % sections}, device_id_type=MESH
        )
    pl.semaphore_wait(barrier, count + 1)
    other = 1 - inner
    side_list = (0, 1)

    def goal(step, side):
        return (outer + (-1 - step if side == 0 else 1 + step) + 2 * ring) % ring

    a_now = {}
    for row, which in ((other, 0), (inner, 1)):
        for side in side_list:
            a_now[which, side] = copies.start(
                part.at[goal(0, side) * 2 + row, rows[side], left],
                a_ring.at[which, side, 0],
                {"ep": sides[side]},
            )
    across = {}
    order = []
    for step in range(ring - 1):
        for side in side_list:
            at = (-1 - step if side == 0 else 1 + step) % ring
            if at not in order:
                order.append(at)
    order.append(0)
    for at in order:
        place = (outer + at) % ring
        across[at] = copies.start(
            part.at[place * 2 + other, :, right], b_across.at[at], {"ep": partner}
        )
    tiny = [
        copies.start(
            prob.at[(me + away) % count], prob_out.at[me], {"ep": (me + away) % count}
        )
        for away in range(1, count)
    ]
    prob_out[me] = prob[me]
    summed = []

    def settle(at):
        if at not in summed:
            summed.append(at)
            across[at].wait_recv()
            place = (outer + at) % ring
            b_across[at] = add(b_across[at], part[place * 2 + inner, :, wide:])

    b_now = {}
    for side in side_list:
        at = (-1 if side == 0 else 1) % ring
        settle(at)
        b_now[side] = copies.start(
            b_across.at[at, rows[side]], b_ring.at[side, 0], {"ep": sides[side]}
        )
    for step in range(ring - 1):
        more = step < ring - 2
        for which, row in ((0, other), (1, inner)):
            for side in side_list:
                place = goal(step + 1, side)
                span = slice(side * half, (side + 1) * half)
                a_now[which, side].wait_recv()
                a_ring[which, side, step] = add(
                    a_ring[which, side, step], part[place * 2 + row, span, :wide]
                )
                if more:
                    a_now[which, side] = copies.start(
                        a_ring.at[which, side, step],
                        a_ring.at[which, side, step + 1],
                        {"ep": sides[side]},
                    )
                elif which == 0:
                    a_now[which, side] = copies.start(
                        a_ring.at[which, side, step], a_take.at[rows[side]], {"ep": partner}
                    )
        for side in side_list:
            at = (-2 - step if side == 0 else 2 + step) % ring
            settle(at)
            span = slice(side * half, (side + 1) * half)
            b_now[side].wait_recv()
            if more:
                b_ring[side, step] = add(b_ring[side, step], b_across[at, span])
                b_now[side] = copies.start(
                    b_ring.at[side, step], b_ring.at[side, step + 1], {"ep": sides[side]}
                )
            else:
                total[1, span] = add(b_ring[side, step], b_across[at, span])

    def shift(column):
        return pltpu.make_async_remote_copy(
            src_ref=total.at[column],
            dst_ref=land.at[column],
            send_sem=shift_send.at[column],
            recv_sem=shift_recv.at[column],
            device_id={"section": (section + sections - 1) % sections},
            device_id_type=MESH,
        )

    @pl.when(section > 0)
    def _():
        shift(1).start()

    for side in side_list:
        span = slice(side * half, (side + 1) * half)
        a_now[0, side].wait_recv()
        total[0, span] = add(a_ring[1, side, ring - 2], a_take[span])

    @pl.when(section > 0)
    def _():
        shift(0).start()

    for copy in tiny:
        copy.wait_recv()
    for copy in copies.items:
        copy.wait_send()

    @pl.when(section > 0)
    def _():
        shift(1).wait_send()
        shift(0).wait_send()

    @pl.when(section < sections - 1)
    def _():
        shift(1).wait_recv()
        out[:, wide:] = land[1]
        shift(0).wait_recv()
        out[:, :wide] = land[0]

    @pl.when(section == sections - 1)
    def _():
        out[...] = jnp.zeros_like(out)


def scatter_tokens(count, sections, part, prob):
    pairs = scatter_copies(count)
    ring = count // 2
    _, tokens, width = part.shape
    half, wide = tokens // 2, width // 2
    return pl.pallas_call(
        functools.partial(scatter_kernel, count, sections),
        out_shape=[
            jax.ShapeDtypeStruct((tokens, width), BF16),
            jax.ShapeDtypeStruct(prob.shape, prob.dtype),
        ],
        in_specs=[VMEM] * 2,
        out_specs=[VMEM] * 2,
        scratch_shapes=[
            pltpu.VMEM((2, 2, ring - 1, half, wide), BF16),
            pltpu.VMEM((2, ring - 1, half, wide), BF16),
            pltpu.VMEM((ring, tokens, wide), BF16),
            pltpu.VMEM((tokens, wide), BF16),
            pltpu.VMEM((2, tokens, wide), BF16),
            pltpu.VMEM((2, tokens, wide), BF16),
            pltpu.SemaphoreType.DMA((pairs,)),
            pltpu.SemaphoreType.DMA((pairs,)),
            pltpu.SemaphoreType.DMA((2,)),
            pltpu.SemaphoreType.DMA((2,)),
        ],
        compiler_params=pltpu.CompilerParams(
            collective_id=1, has_side_effects=True, vmem_limit_bytes=40 * 1024 * 1024
        ),
    )(part, prob)


def per_device(
    output_grad,
    layer_input,
    expert_ids,
    route_probs,
    gate_weight,
    up_weight,
    down_weight,
    saved_inputs,
    saved_gate_grad,
    saved_up_grad,
    saved_counts,
):
    ep_count = lax.axis_size("ep")
    sections = lax.axis_size("section")
    me = lax.axis_index("ep")
    w_gate = gate_weight[0]
    w_up = up_weight[0]
    w_down = down_weight[0]
    local_experts = w_gate.shape[0]
    experts_all = local_experts * ep_count
    slots_all = saved_inputs.shape[2]
    capacity = slots_all // ep_count
    tok_rows = expert_ids.shape[1]
    top_count = expert_ids.shape[2]
    width = output_grad.shape[2]

    small = jnp.concatenate([expert_ids[0].astype(BF16), route_probs[0]], axis=1).T
    grad_all, input_all, small_all = gather_tokens(
        ep_count, output_grad[0], layer_input[0], small
    )

    live = jnp.arange(capacity, dtype=jnp.int32)[None, None, :] < saved_counts[0][:, :, None]
    masked = saved_inputs[0] * live.reshape(local_experts, slots_all).astype(BF16)[:, :, None]
    gate_part = jnp.einsum(
        "esd,esf->edf", masked, saved_gate_grad[0], preferred_element_type=F32
    ).astype(BF16)
    up_part = jnp.einsum(
        "esd,esf->edf", masked, saved_up_grad[0], preferred_element_type=F32
    ).astype(BF16)

    ids_all = small_all[:, :top_count].astype(jnp.int32)
    probs_all = small_all[:, top_count:].astype(F32)
    mine = me * local_experts + jnp.arange(local_experts, dtype=jnp.int32)
    hit = ids_all[:, None, :, :] == mine[None, :, None, None]
    member = jnp.any(hit, axis=2)
    prob = jnp.sum(jnp.where(hit, probs_all[:, None], 0.0), axis=2)
    lower = jnp.tril(jnp.ones((tok_rows, tok_rows), BF16), -1)
    before = jnp.einsum("sen,tn->set", member.astype(BF16), lower, preferred_element_type=F32)
    slot = jnp.where(member, before.astype(jnp.int32), -1)
    chosen = slot[:, :, None, :] == jnp.arange(capacity, dtype=jnp.int32)[None, None, :, None]
    pick = chosen.astype(BF16).reshape(ep_count, local_experts * capacity, tok_rows)
    put = jnp.where(chosen, prob[:, :, None, :], 0.0).astype(BF16)
    put = put.reshape(ep_count, local_experts * capacity, tok_rows)

    def spread(tokens):
        sent = jnp.einsum("spt,std->spd", pick, tokens, preferred_element_type=F32).astype(BF16)
        sent = sent.reshape(ep_count, local_experts, capacity, width)
        return sent.transpose(1, 0, 2, 3).reshape(local_experts, slots_all, width)

    grad_part = spread(grad_all)
    input_part = spread(input_all)

    gate_pre = jnp.einsum("epd,edf->epf", input_part, w_gate, preferred_element_type=F32)
    up_pre = jnp.einsum("epd,edf->epf", input_part, w_up, preferred_element_type=F32)
    sigma = jax.nn.sigmoid(gate_pre)
    active = gate_pre * sigma
    hidden = active * up_pre
    hidden_grad = jnp.einsum("epd,efd->epf", grad_part, w_down, preferred_element_type=F32)
    slot_prob = jnp.sum(hidden_grad * hidden, axis=2).astype(BF16)
    gate_grad = (hidden_grad * up_pre * sigma * (1.0 + gate_pre * (1.0 - sigma))).astype(BF16)
    up_grad = (hidden_grad * active).astype(BF16)
    slot_grad = jnp.einsum("epf,edf->epd", gate_grad, w_gate, preferred_element_type=F32)
    slot_grad = slot_grad + jnp.einsum("epf,edf->epd", up_grad, w_up, preferred_element_type=F32)
    slot_grad = slot_grad.astype(BF16).reshape(local_experts, ep_count, capacity, width)
    slot_grad = slot_grad.transpose(1, 0, 2, 3).reshape(ep_count, -1, width)
    token_grad = jnp.einsum("spt,spd->std", put, slot_grad, preferred_element_type=F32)
    slot_prob = slot_prob.reshape(local_experts, ep_count, capacity)
    by_slot = chosen.astype(BF16)
    token_prob = jnp.einsum("sect,esc->set", by_slot, slot_prob, preferred_element_type=F32)
    upstream, prob_back = scatter_tokens(
        ep_count, sections, token_grad.astype(BF16), token_prob.astype(BF16)
    )
    prob_back = prob_back.reshape(experts_all, tok_rows)
    own = expert_ids[0][None, :, :] == jnp.arange(experts_all, dtype=jnp.int32)[:, None, None]
    prob_part = jnp.sum(jnp.where(own, prob_back[:, :, None].astype(F32), 0.0), axis=0)
    prob_part = prob_part.astype(BF16)
    upstream = upstream[None]
    return (upstream, prob_part[None], gate_part[None], up_part[None])


def solution(mesh):
    three = P("section", "ep", None)
    four = P("section", "ep", None, None)
    return jax.shard_map(
        per_device,
        mesh=mesh,
        in_specs=(three, three, three, three, four, four, four, four, four, four, three),
        out_specs=(three, three, four, four),
        check_vma=False,
    )
```

time: 336 us -> 257 us (0.76)
  waiting for transfers between devices: 217 us -> 0 us
  Pallas kernels: 0 us -> 175 us
  between operations: 14.2 us -> 0.86 us
  matrix products: 74.3 us -> 64.4 us
  local copies, waits for them, and re-layouts: 18.9 us -> 10.3 us
    pallas_call x0 -> x2, Pallas kernels: none -> 175 us  [the longest x1 109 us: gather_tokens(): pl.pallas_call(functools.partial(gather_kernel, count), out_shape=[jax.Sh...]
    all_gather x1 -> x0, waiting for transfers between devices: 129 us -> none  [per_device(): everyone = lax.all_gather(packed, 'ep', axis=0, tiled=False)]
    reduce_scatter x1 -> x0, waiting for transfers between devices: 87.3 us -> none  [per_device(): lax.psum_scatter(back.astype(BF16), 'ep', scatter_dimension=0, tiled=False)]
    convert_element_type x1, local copies, waits for them, and re-layouts: 10 us -> 0.01 us  [per_device(): prob_back[:, :, None].astype(F32)]
    concatenate x3 -> x0, other arithmetic: 5.34 us -> none  [the longest x1 2.32 us: per_device(): jnp.concatenate([token_grad, jnp.pad(spread, ((0, 0), (0, 0), (0, pad)))]...]
    transpose x0 -> x3, local copies, waits for them, and re-layouts: none -> 5.07 us  [the longest x1 3.23 us: per_device(): slot_grad = slot_grad.transpose(1, 0, 2, 3).reshape(ep_count, -1, width)]
    dot_general x3 -> x4, matrix products: 14.5 us -> 10.1 us  [the longest x2 5.26 us: spread(): jnp.einsum('spt,std->spd', pick, tokens, preferred_element_type=F32)]
    dot_general x1, matrix products: 7.16 us -> 2.84 us  [per_device(): jnp.einsum('epd,edf->epf', input_part, w_gate, preferred_element_type=F32)]
  transfers between devices with their start and end apart: 3 -> 0, of which waited for: 2 -> 0; matrix products, arithmetic and copies ran while one was open for 5% -> 0% of each run, Pallas kernels for 0% -> 0%
where the time goes in v2:
time: 257 us; the launch traced here: 255 us
  Pallas kernels  175 us (68%)
  matrix products  64.4 us (25%)
  local copies, waits for them, and re-layouts  10.3 us (4%)
  other arithmetic  4.72 us (2%)
    pallas_call x1, Pallas kernels, gather_tokens(): pl.pallas_call(functools.partial(gather_kernel, count), out_shape=[jax.Sh...  109 us
    pallas_call x1, Pallas kernels, scatter_tokens(): pl.pallas_call(functools.partial(scatter_kernel, count, sections), out_sh...  65.5 us
    dot_general x1, matrix products, per_device(): jnp.einsum('epf,edf->epd', up_grad, w_up, preferred_element_type=F32)  13 us
    dot_general x1, matrix products, per_device(): jnp.einsum('epf,edf->epd', gate_grad, w_gate, preferred_element_type=F32)  11.2 us
    dot_general x1, matrix products, per_device(): jnp.einsum('esd,esf->edf', masked, saved_up_grad[0], preferred_element_ty...  8.2 us
    dot_general x1, matrix products, per_device(): jnp.einsum('esd,esf->edf', masked, saved_gate_grad[0], preferred_element_...  7.63 us
    dot_general x1, matrix products, per_device(): jnp.einsum('epd,efd->epf', grad_part, w_down, preferred_element_type=F32)  6.27 us
    dot_general x2, matrix products, spread(): jnp.einsum('spt,std->spd', pick, tokens, preferred_element_type=F32)  5.26 us

profile of v2, /device:TPU:9, one launch (start us, length us, event | category | flops | bytes accessed | tf_op | source)
XLA Modules:
  0.0 255.0 jit_solution(1453980780887667357)
XLA Ops:
  0.6 0.0 copy-start
  0.6 0.9 bitcast_convert_fusion.1
  1.5 1.4 maximum_bitcast_fusion.s
  2.9 109.3 %shard_map.138 = (bf16[8,256,1024]{2,1,0:T(8,128)(2,1)}, bf16[8,256,1024]{2,1,0:T(8,128)(2,1)}, bf16[8,16,256]{2,1,0:T(8,128)(2,1)}) custom-call(bf16[256,1024]{1,0:T(8,128)(2,1)} %bitcast.89, bf16[256,1024]{1,0:T(8,128)(2,1)} %bitcast.90, bf16[16,256]{1,0:T(8,128)(2,1)} %maximum_bitcast_fusion.s), custom_call_target="tpu_custom_call" | custom-call | tf_op jit(solution)/shard_map/pallas_call | solution.py:127
  112.2 0.8 slice_convert_fusion.1
  113.0 0.2 compare_reduce_fusion
  113.2 0.2 fusion.20
  113.4 0.1 eq.57
  113.5 0.4 bitcast_compare_fusion
  114.0 3.7 %convolution_convert_fusion = bf16[8,320,1024]{2,1,0:T(8,128)(2,1)S(1)} fusion(pred[8,320,256]{2,1,0:T(32,128)(4,1)S(1)} %bitcast_compare_fusion, bf16[8,256,1024]{2,1,0:T(8,128)(2,1)} %get-tuple-element.11), kind=kOutput, calls=%fused_computation.20 | convolution fusion | flops 1344798720 | bytes 10092544 | tf_op jit(solution)/shard_map/spt,std->spd/dot_general | solution.py:386
  117.7 0.9 copy.30
  118.6 0.0 copy-done
  118.7 0.0 copy-start.9
  118.7 2.8 %fusion.5 = f32[4,640,384]{1,2,0:T(8,128)S(1)} fusion(bf16[4,640,1024]{2,1,0:T(8,128)(2,1)S(1)} %bitcast.87, bf16[1,4,1024,384]{3,2,1,0:T(8,128)(2,1)S(1)} %copy-done), kind=kOutput, calls=%fused_computation.11 | convolution fusion | flops 2013265920 | bytes 12320768 | tf_op jit(solution)/shard_map/epd,edf->epf/dot_general | solution.py:393
  121.5 0.0 copy-done.9
  121.5 0.0 copy-start.11
  121.5 0.0 copy-start.5
  121.5 4.9 %fusion.8 = f32[4,640,384]{1,2,0:T(8,128)} fusion(bf16[4,640,1024]{2,1,0:T(8,128)(2,1)S(1)} %bitcast.88, bf16[1,4,1024,384]{3,2,1,0:T(8,128)(2,1)S(1)} %copy-done.9), kind=kOutput, calls=%fused_computation.14 | convolution fusion | flops 2013265920 | bytes 12320768 | tf_op jit(solution)/shard_map/epd,edf->epf/dot_general | solution.py:394
  126.4 0.0 copy-done.5
  126.4 1.5 convolution_convert_fusion.1
  128.0 0.0 copy-start.8
  128.0 0.9 copy.29
  128.9 0.9 copy-done.8
  129.8 6.3 %multiply_reduce_fusion = (bf16[4,640]{1,0:T(4,128)(2,1)S(1)}, f32[4,640,384]{1,2,0:T(8,128)}) fusion(f32[4,640,384]{1,2,0:T(8,128)} %fusion.8, f32[4,640,384]{1,2,0:T(8,128)S(1)} %fusion.5, bf16[4,640,1024]{2,1,0:T(8,128)(2,1)S(1)} %bitcast.85, bf16[1,4,384,1024]{3,2,1,0:T(8,128)(2,1)S(1)} %copy-done.8), kind=kOutput, calls=%fused_computation.4 | convolution fusion | flops 2020144640 | bytes 20190208 | tf_op jit(solution)/shard_map/epd,efd->epf/dot_general | solution.py:398
  136.1 0.0 copy-done.11
  136.1 11.2 %fusion.3 = f32[4,640,1024]{2,1,0:T(8,128)} fusion(bf16[1,4,1024,384]{3,2,1,0:T(8,128)(2,1)S(1)} %copy-done, f32[4,640,384]{1,2,0:T(8,128)S(1)} %fusion.5, f32[4,640,384]{1,2,0:T(8,128)} %get-tuple-element.17, f32[4,640,384]{1,2,0:T(8,128)} %fusion.8), kind=kOutput, calls=%fused_computation.9 | convolution fusion | flops 2023096320 | bytes 25427968 | tf_op jit(solution)/shard_map/epf,edf->epd/dot_general | solution.py:402
  147.3 13.0 %add_convert_fusion = bf16[4,640,1024]{2,1,0:T(8,128)(2,1)} fusion(f32[4,640,1024]{2,1,0:T(8,128)} %fusion.3, bf16[1,4,1024,384]{3,2,1,0:T(8,128)(2,1)} %param.16, f32[4,640,384]{1,2,0:T(8,128)} %get-tuple-element.17, f32[4,640,384]{1,2,0:T(8,128)} %copy-done.11), kind=kOutput, calls=%fused_computation | convolution fusion | flops 2024407040 | bytes 26738688 | tf_op jit(solution)/shard_map/epf,edf->epd/dot_general | solution.py:403
  160.4 3.2 %copy.35 = bf16[8,4,80,1024]{3,2,1,0:T(8,128)(2,1)S(1)} copy(bf16[8,4,80,1024]{3,2,0,1:T(8,128)(2,1)} %bitcast.86) | data formatting | bytes 10485760 | tf_op jit(solution)/shard_map/transpose | solution.py:405
  163.6 0.2 fusion.22
  163.8 0.3 fusion.12
  164.0 4.3 %convolution_convert_fusion.2.part = bf16[8,256,1024]{2,1,0:T(8,128)(2,1)} fusion(bf16[8,320,256]{2,1,0:T(8,128)(2,1)S(1)} %fusion.12, bf16[8,320,1024]{2,1,0:T(8,128)(2,1)S(1)} %bitcast.82), kind=kOutput, calls=%fused_computation.22 | convolution fusion | flops 1344274432 | bytes 10747904 | tf_op jit(solution)/shard_map/spt,spd->std/dot_general | solution.py:406
  168.4 0.0 copy-start.6
  168.4 0.0 copy-start.7
  168.4 0.1 reshape.92
  168.4 0.5 fusion.15
  169.0 0.0 copy-start.2
  169.0 2.2 copy-done.2
  171.2 65.5 %shard_map.139 = (bf16[256,1024]{1,0:T(8,128)(2,1)S(1)}, bf16[8,4,256]{2,1,0:T(4,128)(2,1)S(1)}) custom-call(bf16[8,256,1024]{2,1,0:T(8,128)(2,1)S(1)} %copy-done.2, bf16[8,4,256]{2,1,0:T(4,128)(2,1)S(1)} %bitcast.81), custom_call_target="tpu_custom_call" | custom-call | tf_op jit(solution)/shard_map/pallas_call | solution.py:304
  236.7 0.0 copy-start.3
  236.7 0.8 copy-done.3
  237.5 0.0 copy-done.6
  237.5 0.6 select_reduce_fusion
  238.1 0.0 copy-done.7
  238.1 0.1 lt.30
  238.2 0.1 lt.31
  238.3 0.1 lt.27
  238.4 0.0 copy-start.10
  238.4 8.2 %convert_bitcast_fusion = bf16[1,4,1024,384]{3,2,1,0:T(8,128)(2,1)} fusion(bf16[1,4,640,1024]{3,2,1,0:T(8,128)(2,1)} %param.18, bf16[4,640]{1,0:T(4,128)(2,1)S(1)} %compare_convert_fusion, bf16[1,4,640,384]{3,2,1,0:T(8,128)(2,1)} %param.20), kind=kOutput, calls=%fused_computation.18 | convolution fusion | flops 2017460224 | bytes 10359808 | tf_op jit(solution)/shard_map/esd,esf->edf/dot_general | solution.py:367
  246.6 0.0 copy-done.10
  246.6 0.0 copy-start.4
  246.6 0.0 copy-start.1
  246.6 7.6 %convert_bitcast_fusion.1 = bf16[1,4,1024,384]{3,2,1,0:T(8,128)(2,1)} fusion(bf16[1,4,640,1024]{3,2,1,0:T(8,128)(2,1)} %param.18, bf16[4,640]{1,0:T(4,128)(2,1)S(1)} %compare_convert_fusion, bf16[1,4,640,384]{3,2,1,0:T(8,128)(2,1)S(1)} %copy-done.10), kind=kOutput, calls=%fused_computation.19 | convolution fusion | flops 2017460224 | bytes 10359808 | tf_op jit(solution)/shard_map/esd,esf->edf/dot_general | solution.py:364
  254.2 0.0 copy-done.4
  254.2 0.8 copy.56
  255.0 0.0 copy-done.1
  (8 shorter events, 0.1 us)
Async XLA Ops:
  0.6 118.0 %copy-start = (bf16[1,4,1024,384]{3,2,1,0:T(8,128)(2,1)S(1)}, bf16[1,4,1024,384]{3,2,1,0:T(8,128)(2,1)}, u32[]{:S(2)}) copy-start(bf16[1,4,1024,384]{3,2,1,0:T(8,128)(2,1)} %param.15) | copy-start | bytes 9437188
  118.7 2.9 %copy-start.9 = (bf16[1,4,1024,384]{3,2,1,0:T(8,128)(2,1)S(1)}, bf16[1,4,1024,384]{3,2,1,0:T(8,128)(2,1)}, u32[]{:S(2)}) copy-start(bf16[1,4,1024,384]{3,2,1,0:T(8,128)(2,1)} %param.16) | copy-start | bytes 9437188
  121.5 14.6 %copy-start.11 = (f32[4,640,384]{1,2,0:T(8,128)}, f32[4,640,384]{1,2,0:T(8,128)S(1)}, u32[]{:S(2)}) copy-start(f32[4,640,384]{1,2,0:T(8,128)S(1)} %fusion.5) | copy-start | bytes 11796484
  121.5 4.9 %copy-start.5 = (bf16[8,256,1024]{2,1,0:T(8,128)(2,1)S(1)}, bf16[8,256,1024]{2,1,0:T(8,128)(2,1)}, u32[]{:S(2)}) copy-start(bf16[8,256,1024]{2,1,0:T(8,128)(2,1)} %get-tuple-element.10) | copy-start | bytes 12582916
  128.0 1.9 copy-start.8
  168.4 69.1 %copy-start.6 = (s32[1,256,8]{1,2,0:T(8,128)S(1)}, s32[1,256,8]{1,2,0:T(8,128)}, u32[]{:S(2)}) copy-start(s32[1,256,8]{1,2,0:T(8,128)} %param.13) | copy-start | bytes 24580
  168.4 69.8 %copy-start.7 = (s32[1,4,8]{2,1,0:T(4,128)S(1)}, s32[1,4,8]{2,1,0:T(4,128)}, u32[]{:S(2)}) copy-start(s32[1,4,8]{2,1,0:T(4,128)} %param.21) | copy-start | bytes 388
  169.0 2.2 copy-start.2
  236.7 0.8 copy-start.3
  238.4 8.2 %copy-start.10 = (bf16[1,4,640,384]{3,2,1,0:T(8,128)(2,1)S(1)}, bf16[1,4,640,384]{3,2,1,0:T(8,128)(2,1)}, u32[]{:S(2)}) copy-start(bf16[1,4,640,384]{3,2,1,0:T(8,128)(2,1)} %param.19) | copy-start | bytes 5898244
  246.6 7.6 %copy-start.4 = (bf16[256,1024]{1,0:T(8,128)(2,1)S(1)}, bf16[256,1024]{1,0:T(8,128)(2,1)}, u32[]{:S(2)}) copy-start(bf16[256,1024]{1,0:T(8,128)(2,1)} %copy-done.3) | copy-start | bytes 1572868
  246.6 8.4 %copy-start.1 = (bf16[1,4,1024,384]{3,2,1,0:T(8,128)(2,1)S(1)}, bf16[1,4,1024,384]{3,2,1,0:T(8,128)(2,1)}, u32[]{:S(2)}) copy-start(bf16[1,4,1024,384]{3,2,1,0:T(8,128)(2,1)} %param.15) | copy-start | bytes 9437188

commit v3 on v2

v3 whole, which is shorter than its diff:
```python
import functools

import jax
import jax.numpy as jnp
from jax import lax
from jax.experimental import pallas as pl
from jax.experimental.pallas import tpu as pltpu
from jax.sharding import PartitionSpec as P

F32 = jnp.float32
BF16 = jnp.bfloat16
MESH = pl.DeviceIdType.MESH
VMEM = pl.BlockSpec(memory_space=pltpu.VMEM)
ANY = pl.BlockSpec(memory_space=pl.ANY)


class Copies:
    def __init__(self, send, recv):
        self.send, self.recv, self.used, self.items = send, recv, 0, []

    def start(self, src, dst, target, when=None):
        at = self.used
        self.used += 1
        copy = pltpu.make_async_remote_copy(
            src_ref=src,
            dst_ref=dst,
            send_sem=self.send.at[at],
            recv_sem=self.recv.at[at],
            device_id={"ep": target},
            device_id_type=MESH,
        )
        self.items.append((copy, when))
        guarded(when, copy.start)
        return copy

    def finish(self):
        for copy, when in self.items:
            guarded(when, copy.wait_send)


def guarded(when, act):
    if when is None:
        act()
    else:
        pl.when(when)(act)


def place_of(count):
    me = lax.axis_index("ep")
    outer, inner = me // 2, me % 2
    line = count // 2
    up = ((outer + 1) % line) * 2 + inner
    down = ((outer + line - 1) % line) * 2 + inner
    return me, outer, inner, line, (up, down), outer * 2 + 1 - inner


def gather_copies(count):
    line = count // 2
    return 12 * (line - 1) + 3 + (count - 1)


def gather_kernel(count, g, x, s, g_all, x_all, s_all, local, send, recv):
    me, outer, inner, line, sides, partner = place_of(count)
    width = g.shape[1]
    cut = max(width * 3 // 1024, 1) * 128
    copies = Copies(send, recv)
    own = [
        pltpu.make_async_copy(g, g_all.at[me], local.at[0]),
        pltpu.make_async_copy(x, x_all.at[me], local.at[1]),
        pltpu.make_async_copy(s, s_all.at[me], local.at[2]),
    ]
    for copy in own:
        copy.start()
    barrier = pltpu.get_barrier_semaphore()
    for away in range(1, count):
        pl.semaphore_signal(
            barrier, inc=1, device_id={"ep": (me + away) % count}, device_id_type=MESH
        )
    pl.semaphore_wait(barrier, count - 1)
    everything, few, many = pl.ds(0, width), pl.ds(0, cut), pl.ds(cut, width - cut)

    def block(step, side):
        return (outer + (-step if side == 0 else step) + 2 * line) % line

    def arrives(step, side):
        return outer >= step + 1 if side == 0 else outer + step + 1 <= line - 1

    def leaves(step, side):
        if side == 0:
            return jnp.logical_and(outer >= step, outer < line - 1)
        return jnp.logical_and(outer + step <= line - 1, outer > 0)

    def hop(ref, all_ref, columns, step, side, row):
        dst = all_ref.at[block(step, side) * 2 + row, :, columns]
        source = dst if ref is None else ref.at[:, columns]
        return copies.start(source, dst, sides[side], leaves(step, side))

    def take(copy, step, side):
        guarded(arrives(step, side), copy.wait_recv)

    side_list = (0, 1)
    other = 1 - inner
    pieces = ((x, x_all, everything), (g, g_all, many))
    now = {}
    g_across = copies.start(g.at[:, few], g_all.at[me, :, few], partner)
    for at, (ref, all_ref, columns) in enumerate(pieces):
        for side in side_list:
            now[at, side] = hop(ref, all_ref, columns, 0, side, inner)
    for side in side_list:
        now[2, side] = hop(g, g_all, few, 0, side, inner)
    late = [
        (copies.start(x, x_all.at[me], partner), None),
        (copies.start(g.at[:, many], g_all.at[me, :, many], partner), None),
    ]
    for away in range(1, count):
        late.append((copies.start(s, s_all.at[me], (me + away) % count), None))
    g_across.wait_recv()
    for side in side_list:
        now[3, side] = hop(None, g_all, few, 0, side, other)
    for step in range(line - 1):
        more = step < line - 2
        for at in range(4):
            row = other if at == 3 else inner
            all_ref, columns = pieces[at][1:] if at < 2 else (g_all, few)
            for side in side_list:
                take(now[at, side], step, side)
                if more:
                    now[at, side] = hop(None, all_ref, columns, step + 1, side, row)
                if at < 2:
                    got = all_ref.at[block(step + 1, side) * 2 + inner, :, columns]
                    has = arrives(step, side)
                    late.append((copies.start(got, got, partner, has), has))
    for copy, when in late:
        guarded(when, copy.wait_recv)
    copies.finish()
    for copy in own:
        copy.wait()


def gather_tokens(count, g, x, s):
    pairs = gather_copies(count)
    return pl.pallas_call(
        functools.partial(gather_kernel, count),
        out_shape=[jax.ShapeDtypeStruct((count,) + a.shape, a.dtype) for a in (g, x, s)],
        in_specs=[VMEM] * 3,
        out_specs=[ANY] * 3,
        scratch_shapes=[
            pltpu.SemaphoreType.DMA((3,)),
            pltpu.SemaphoreType.DMA((pairs,)),
            pltpu.SemaphoreType.DMA((pairs,)),
        ],
        compiler_params=pltpu.CompilerParams(collective_id=0, has_side_effects=True),
    )(g, x, s)


def scatter_copies(count):
    line = count // 2
    return line + 1 + (count - 1)


def add(a, b):
    return (a.astype(F32) + b.astype(F32)).astype(BF16)


def scatter_kernel(
    count, sections, part, prob, out, prob_out, a_sum, a_side, a_take, b_sum, b_side, land_a,
    land_b, send, recv, line_send, line_recv, shift_send, shift_recv,
):
    me, outer, inner, line, sides, partner = place_of(count)
    section = lax.axis_index("section")
    cut = a_sum.shape[3]
    copies = Copies(send, recv)
    barrier = pltpu.get_barrier_semaphore()
    for away in range(1, count):
        pl.semaphore_signal(
            barrier, inc=1, device_id={"ep": (me + away) % count}, device_id_type=MESH
        )
    for away in (1, sections - 1):
        pl.semaphore_signal(
            barrier, inc=1, device_id={"section": (section + away) % sections}, device_id_type=MESH
        )
    pl.semaphore_wait(barrier, count + 1)
    other = 1 - inner
    low, high = pl.ds(0, cut), pl.ds(cut, part.shape[2] - cut)

    def goal(at):
        mixed = line - 1 - at // 2 if at % 2 == 0 else at // 2
        return jnp.where(outer == 0, line - 1 - at, jnp.where(outer == line - 1, at, mixed))

    across = [
        copies.start(part.at[goal(at) * 2 + other, :, high], b_sum.at[goal(at)], partner)
        for at in range(line)
    ]
    tiny = [
        copies.start(prob.at[(me + away) % count], prob_out.at[me], (me + away) % count)
        for away in range(1, count)
    ]
    prob_out[me] = prob[me]

    def line_copy(kind, source, side_ref, side, place):
        return pltpu.make_async_remote_copy(
            src_ref=source.at[place],
            dst_ref=side_ref.at[side, place],
            send_sem=line_send.at[kind, side, place],
            recv_sem=line_recv.at[kind, side, place],
            device_id={"ep": sides[side]},
            device_id_type=MESH,
        )

    def collect(kind, total, side_ref, side, place):
        line_copy(kind, total, side_ref, side, place).wait_recv()
        total[place] = add(total[place], side_ref[side, place])

    def advance(kind, total, side_ref, place):
        @pl.when(jnp.logical_and(place >= outer, outer > 0))
        def _():
            collect(kind, total, side_ref, 0, place)

        @pl.when(jnp.logical_and(place <= outer, outer < line - 1))
        def _():
            collect(kind, total, side_ref, 1, place)

        @pl.when(place > outer)
        def _():
            line_copy(kind, total, side_ref, 0, place).start()

        @pl.when(place < outer)
        def _():
            line_copy(kind, total, side_ref, 1, place).start()

    for at in range(line):
        place = goal(at)
        for kind, row in ((0, other), (1, inner)):
            a_sum[kind, place] = part[place * 2 + row, :, :cut]
            advance(kind, a_sum.at[kind], a_side.at[kind], place)
    a_across = copies.start(a_sum.at[0, outer], a_take, partner)
    for at in range(line):
        place = goal(at)
        across[at].wait_recv()
        b_sum[place] = add(b_sum[place], part[place * 2 + inner, :, cut:])
        advance(2, b_sum, b_side, place)

    def shift(column, source, land):
        return pltpu.make_async_remote_copy(
            src_ref=source,
            dst_ref=land,
            send_sem=shift_send.at[column],
            recv_sem=shift_recv.at[column],
            device_id={"section": (section + sections - 1) % sections},
            device_id_type=MESH,
        )

    a_across.wait_recv()
    a_sum[1, outer] = add(a_sum[1, outer], a_take[...])
    shifts = (shift(0, a_sum.at[1, outer], land_a), shift(1, b_sum.at[outer], land_b))

    @pl.when(section > 0)
    def _():
        for copy in shifts:
            copy.start()

    for copy in tiny:
        copy.wait_recv()
    copies.finish()
    for place in range(line):
        for kind, total, side_ref in (
            (0, a_sum.at[0], a_side.at[0]),
            (1, a_sum.at[1], a_side.at[1]),
            (2, b_sum, b_side),
        ):
            guarded(place > outer, line_copy(kind, total, side_ref, 0, place).wait_send)
            guarded(place < outer, line_copy(kind, total, side_ref, 1, place).wait_send)

    @pl.when(section > 0)
    def _():
        for copy in shifts:
            copy.wait_send()

    @pl.when(section < sections - 1)
    def _():
        shifts[0].wait_recv()
        out[:, :cut] = land_a[...]
        shifts[1].wait_recv()
        out[:, cut:] = land_b[...]

    @pl.when(section == sections - 1)
    def _():
        out[...] = jnp.zeros_like(out)


def scatter_tokens(count, sections, part, prob):
    pairs = scatter_copies(count)
    line = count // 2
    _, tokens, width = part.shape
    cut = max(width // 1024, 1) * 128
    rest = width - cut
    return pl.pallas_call(
        functools.partial(scatter_kernel, count, sections),
        out_shape=[
            jax.ShapeDtypeStruct((tokens, width), BF16),
            jax.ShapeDtypeStruct(prob.shape, prob.dtype),
        ],
        in_specs=[VMEM] * 2,
        out_specs=[VMEM] * 2,
        scratch_shapes=[
            pltpu.VMEM((2, line, tokens, cut), BF16),
            pltpu.VMEM((2, 2, line, tokens, cut), BF16),
            pltpu.VMEM((tokens, cut), BF16),
            pltpu.VMEM((line, tokens, rest), BF16),
            pltpu.VMEM((2, line, tokens, rest), BF16),
            pltpu.VMEM((tokens, cut), BF16),
            pltpu.VMEM((tokens, rest), BF16),
            pltpu.SemaphoreType.DMA((pairs,)),
            pltpu.SemaphoreType.DMA((pairs,)),
            pltpu.SemaphoreType.DMA((3, 2, line)),
            pltpu.SemaphoreType.DMA((3, 2, line)),
            pltpu.SemaphoreType.DMA((2,)),
            pltpu.SemaphoreType.DMA((2,)),
        ],
        compiler_params=pltpu.CompilerParams(
            collective_id=1, has_side_effects=True, vmem_limit_bytes=48 * 1024 * 1024
        ),
    )(part, prob)


def per_device(
    output_grad,
    layer_input,
    expert_ids,
    route_probs,
    gate_weight,
    up_weight,
    down_weight,
    saved_inputs,
    saved_gate_grad,
    saved_up_grad,
    saved_counts,
):
    ep_count = lax.axis_size("ep")
    sections = lax.axis_size("section")
    me = lax.axis_index("ep")
    w_gate = gate_weight[0]
    w_up = up_weight[0]
    w_down = down_weight[0]
    local_experts = w_gate.shape[0]
    experts_all = local_experts * ep_count
    slots_all = saved_inputs.shape[2]
    capacity = slots_all // ep_count
    tok_rows = expert_ids.shape[1]
    top_count = expert_ids.shape[2]
    width = output_grad.shape[2]

    small = jnp.concatenate([expert_ids[0].astype(BF16), route_probs[0]], axis=1).T
    grad_all, input_all, small_all = gather_tokens(
        ep_count, output_grad[0], layer_input[0], small
    )

    live = jnp.arange(capacity, dtype=jnp.int32)[None, None, :] < saved_counts[0][:, :, None]
    masked = saved_inputs[0] * live.reshape(local_experts, slots_all).astype(BF16)[:, :, None]
    gate_part = jnp.einsum(
        "esd,esf->edf", masked, saved_gate_grad[0], preferred_element_type=F32
    ).astype(BF16)
    up_part = jnp.einsum(
        "esd,esf->edf", masked, saved_up_grad[0], preferred_element_type=F32
    ).astype(BF16)

    ids_all = small_all[:, :top_count].astype(jnp.int32)
    probs_all = small_all[:, top_count:].astype(F32)
    mine = me * local_experts + jnp.arange(local_experts, dtype=jnp.int32)
    hit = ids_all[:, None, :, :] == mine[None, :, None, None]
    member = jnp.any(hit, axis=2)
    prob = jnp.sum(jnp.where(hit, probs_all[:, None], 0.0), axis=2)
    lower = jnp.tril(jnp.ones((tok_rows, tok_rows), BF16), -1)
    before = jnp.einsum("sen,tn->set", member.astype(BF16), lower, preferred_element_type=F32)
    slot = jnp.where(member, before.astype(jnp.int32), -1)
    chosen = slot[:, :, None, :] == jnp.arange(capacity, dtype=jnp.int32)[None, None, :, None]
    pick = chosen.astype(BF16).reshape(ep_count, local_experts * capacity, tok_rows)
    put = jnp.where(chosen, prob[:, :, None, :], 0.0).astype(BF16)
    put = put.reshape(ep_count, local_experts * capacity, tok_rows)

    def spread(tokens):
        sent = jnp.einsum("spt,std->spd", pick, tokens, preferred_element_type=F32).astype(BF16)
        sent = sent.reshape(ep_count, local_experts, capacity, width)
        return sent.transpose(1, 0, 2, 3).reshape(local_experts, slots_all, width)

    grad_part = spread(grad_all)
    input_part = spread(input_all)

    gate_pre = jnp.einsum("epd,edf->epf", input_part, w_gate, preferred_element_type=F32)
    up_pre = jnp.einsum("epd,edf->epf", input_part, w_up, preferred_element_type=F32)
    sigma = jax.nn.sigmoid(gate_pre)
    active = gate_pre * sigma
    hidden = active * up_pre
    hidden_grad = jnp.einsum("epd,efd->epf", grad_part, w_down, preferred_element_type=F32)
    slot_prob = jnp.sum(hidden_grad * hidden, axis=2).astype(BF16)
    gate_grad = (hidden_grad * up_pre * sigma * (1.0 + gate_pre * (1.0 - sigma))).astype(BF16)
    up_grad = (hidden_grad * active).astype(BF16)
    slot_grad = jnp.einsum("epf,edf->epd", gate_grad, w_gate, preferred_element_type=F32)
    slot_grad = slot_grad + jnp.einsum("epf,edf->epd", up_grad, w_up, preferred_element_type=F32)
    slot_grad = slot_grad.astype(BF16).reshape(local_experts, ep_count, capacity, width)
    slot_grad = slot_grad.transpose(1, 0, 2, 3).reshape(ep_count, -1, width)
    token_grad = jnp.einsum("spt,spd->std", put, slot_grad, preferred_element_type=F32)
    slot_prob = slot_prob.reshape(local_experts, ep_count, capacity)
    by_slot = chosen.astype(BF16)
    token_prob = jnp.einsum("sect,esc->set", by_slot, slot_prob, preferred_element_type=F32)
    upstream, prob_back = scatter_tokens(
        ep_count, sections, token_grad.astype(BF16), token_prob.astype(BF16)
    )
    prob_back = prob_back.reshape(experts_all, tok_rows)
    own = expert_ids[0][None, :, :] == jnp.arange(experts_all, dtype=jnp.int32)[:, None, None]
    prob_part = jnp.sum(jnp.where(own, prob_back[:, :, None].astype(F32), 0.0), axis=0)
    prob_part = prob_part.astype(BF16)
    upstream = upstream[None]
    return (upstream, prob_part[None], gate_part[None], up_part[None])


def solution(mesh):
    three = P("section", "ep", None)
    four = P("section", "ep", None, None)
    return jax.shard_map(
        per_device,
        mesh=mesh,
        in_specs=(three, three, three, three, four, four, four, four, four, four, three),
        out_specs=(three, three, four, four),
        check_vma=False,
    )
```

time: 257 us -> 244 us (0.949)
  Pallas kernels: 175 us -> 163 us
    pallas_call x1, Pallas kernels: 109 us -> 85.9 us  [gather_tokens(): pl.pallas_call(functools.partial(gather_kernel, count), out_shape=[jax.Sh...]
    pallas_call x1, Pallas kernels: 65.5 us -> 77.4 us  [scatter_tokens(): pl.pallas_call(functools.partial(scatter_kernel, count, sections), out_sh...]
where the time goes in v3:
time: 244 us
  Pallas kernels  163 us (67%)
  matrix products  64.4 us (26%)
  local copies, waits for them, and re-layouts  10.3 us (4%)
  other arithmetic  4.72 us (2%)
    pallas_call x1, Pallas kernels, gather_tokens(): pl.pallas_call(functools.partial(gather_kernel, count), out_shape=[jax.Sh...  85.9 us
    pallas_call x1, Pallas kernels, scatter_tokens(): pl.pallas_call(functools.partial(scatter_kernel, count, sections), out_sh...  77.4 us
    dot_general x1, matrix products, per_device(): jnp.einsum('epf,edf->epd', up_grad, w_up, preferred_element_type=F32)  13 us
    dot_general x1, matrix products, per_device(): jnp.einsum('epf,edf->epd', gate_grad, w_gate, preferred_element_type=F32)  11.2 us
    dot_general x1, matrix products, per_device(): jnp.einsum('esd,esf->edf', masked, saved_up_grad[0], preferred_element_ty...  8.2 us
    dot_general x1, matrix products, per_device(): jnp.einsum('esd,esf->edf', masked, saved_gate_grad[0], preferred_element_...  7.63 us
    dot_general x1, matrix products, per_device(): jnp.einsum('epd,efd->epf', grad_part, w_down, preferred_element_type=F32)  6.27 us
    dot_general x2, matrix products, spread(): jnp.einsum('spt,std->spd', pick, tokens, preferred_element_type=F32)  5.27 us

profile of v3, /device:TPU:9, one launch (start us, length us, event | category | flops | bytes accessed | tf_op | source)
XLA Modules:
  0.0 243.5 jit_solution(2225228847166841974)
XLA Ops:
  0.6 0.0 copy-start
  0.6 0.9 bitcast_convert_fusion.1
  1.5 1.4 maximum_bitcast_fusion.s
  2.9 85.9 %shard_map.138 = (bf16[8,256,1024]{2,1,0:T(8,128)(2,1)}, bf16[8,256,1024]{2,1,0:T(8,128)(2,1)}, bf16[8,16,256]{2,1,0:T(8,128)(2,1)}) custom-call(bf16[256,1024]{1,0:T(8,128)(2,1)} %bitcast.89, bf16[256,1024]{1,0:T(8,128)(2,1)} %bitcast.90, bf16[16,256]{1,0:T(8,128)(2,1)} %maximum_bitcast_fusion.s), custom_call_target="tpu_custom_call" | custom-call | tf_op jit(solution)/shard_map/pallas_call | solution.py:142
  88.8 0.8 slice_convert_fusion.1
  89.6 0.2 compare_reduce_fusion
  89.8 0.2 fusion.20
  90.1 0.1 eq.57
  90.1 0.4 bitcast_compare_fusion
  90.6 3.7 %convolution_convert_fusion = bf16[8,320,1024]{2,1,0:T(8,128)(2,1)S(1)} fusion(pred[8,320,256]{2,1,0:T(32,128)(4,1)S(1)} %bitcast_compare_fusion, bf16[8,256,1024]{2,1,0:T(8,128)(2,1)} %get-tuple-element.11), kind=kOutput, calls=%fused_computation.20 | convolution fusion | flops 1344798720 | bytes 10092544 | tf_op jit(solution)/shard_map/spt,std->spd/dot_general | solution.py:382
  94.3 0.9 copy.30
  95.3 0.0 copy-done
  95.3 0.0 copy-start.9
  95.3 2.8 %fusion.5 = f32[4,640,384]{1,2,0:T(8,128)S(1)} fusion(bf16[4,640,1024]{2,1,0:T(8,128)(2,1)S(1)} %bitcast.87, bf16[1,4,1024,384]{3,2,1,0:T(8,128)(2,1)S(1)} %copy-done), kind=kOutput, calls=%fused_computation.11 | convolution fusion | flops 2013265920 | bytes 12320768 | tf_op jit(solution)/shard_map/epd,edf->epf/dot_general | solution.py:389
  98.1 0.0 copy-done.9
  98.2 0.0 copy-start.11
  98.2 0.0 copy-start.5
  98.2 4.9 %fusion.8 = f32[4,640,384]{1,2,0:T(8,128)} fusion(bf16[4,640,1024]{2,1,0:T(8,128)(2,1)S(1)} %bitcast.88, bf16[1,4,1024,384]{3,2,1,0:T(8,128)(2,1)S(1)} %copy-done.9), kind=kOutput, calls=%fused_computation.14 | convolution fusion | flops 2013265920 | bytes 12320768 | tf_op jit(solution)/shard_map/epd,edf->epf/dot_general | solution.py:390
  103.0 0.0 copy-done.5
  103.0 1.5 convolution_convert_fusion.1
  104.6 0.0 copy-start.8
  104.6 0.9 copy.29
  105.5 0.9 copy-done.8
  106.5 6.3 %multiply_reduce_fusion = (bf16[4,640]{1,0:T(4,128)(2,1)S(1)}, f32[4,640,384]{1,2,0:T(8,128)}) fusion(f32[4,640,384]{1,2,0:T(8,128)} %fusion.8, f32[4,640,384]{1,2,0:T(8,128)S(1)} %fusion.5, bf16[4,640,1024]{2,1,0:T(8,128)(2,1)S(1)} %bitcast.85, bf16[1,4,384,1024]{3,2,1,0:T(8,128)(2,1)S(1)} %copy-done.8), kind=kOutput, calls=%fused_computation.4 | convolution fusion | flops 2020144640 | bytes 20190208 | tf_op jit(solution)/shard_map/epd,efd->epf/dot_general | solution.py:394
  112.7 0.0 copy-done.11
  112.7 11.2 %fusion.3 = f32[4,640,1024]{2,1,0:T(8,128)} fusion(bf16[1,4,1024,384]{3,2,1,0:T(8,128)(2,1)S(1)} %copy-done, f32[4,640,384]{1,2,0:T(8,128)S(1)} %fusion.5, f32[4,640,384]{1,2,0:T(8,128)} %get-tuple-element.17, f32[4,640,384]{1,2,0:T(8,128)} %fusion.8), kind=kOutput, calls=%fused_computation.9 | convolution fusion | flops 2023096320 | bytes 25427968 | tf_op jit(solution)/shard_map/epf,edf->epd/dot_general | solution.py:398
  124.0 13.0 %add_convert_fusion = bf16[4,640,1024]{2,1,0:T(8,128)(2,1)} fusion(f32[4,640,1024]{2,1,0:T(8,128)} %fusion.3, bf16[1,4,1024,384]{3,2,1,0:T(8,128)(2,1)} %param.16, f32[4,640,384]{1,2,0:T(8,128)} %get-tuple-element.17, f32[4,640,384]{1,2,0:T(8,128)} %copy-done.11), kind=kOutput, calls=%fused_computation | convolution fusion | flops 2024407040 | bytes 26738688 | tf_op jit(solution)/shard_map/epf,edf->epd/dot_general | solution.py:399
  137.0 3.2 %copy.35 = bf16[8,4,80,1024]{3,2,1,0:T(8,128)(2,1)S(1)} copy(bf16[8,4,80,1024]{3,2,0,1:T(8,128)(2,1)} %bitcast.86) | data formatting | bytes 10485760 | tf_op jit(solution)/shard_map/transpose | solution.py:401
  140.2 0.2 fusion.22
  140.4 0.3 fusion.12
  140.7 4.3 %convolution_convert_fusion.2.part = bf16[8,256,1024]{2,1,0:T(8,128)(2,1)} fusion(bf16[8,320,256]{2,1,0:T(8,128)(2,1)S(1)} %fusion.12, bf16[8,320,1024]{2,1,0:T(8,128)(2,1)S(1)} %bitcast.82), kind=kOutput, calls=%fused_computation.22 | convolution fusion | flops 1344274432 | bytes 10747904 | tf_op jit(solution)/shard_map/spt,spd->std/dot_general | solution.py:402
  145.0 0.0 copy-start.6
  145.0 0.0 copy-start.7
  145.0 0.1 reshape.92
  145.1 0.5 fusion.15
  145.6 0.0 copy-start.2
  145.6 2.2 copy-done.2
  147.8 77.4 %shard_map.139 = (bf16[256,1024]{1,0:T(8,128)(2,1)S(1)}, bf16[8,4,256]{2,1,0:T(4,128)(2,1)S(1)}) custom-call(bf16[8,256,1024]{2,1,0:T(8,128)(2,1)S(1)} %copy-done.2, bf16[8,4,256]{2,1,0:T(4,128)(2,1)S(1)} %bitcast.81), custom_call_target="tpu_custom_call" | custom-call | tf_op jit(solution)/shard_map/pallas_call | solution.py:297
  225.2 0.0 copy-start.3
  225.2 0.8 copy-done.3
  226.0 0.0 copy-done.6
  226.0 0.6 select_reduce_fusion
  226.6 0.0 copy-done.7
  226.6 0.1 lt.30
  226.7 0.1 lt.31
  226.8 0.1 lt.27
  226.9 0.0 copy-start.10
  226.9 8.2 %convert_bitcast_fusion = bf16[1,4,1024,384]{3,2,1,0:T(8,128)(2,1)} fusion(bf16[1,4,640,1024]{3,2,1,0:T(8,128)(2,1)} %param.18, bf16[4,640]{1,0:T(4,128)(2,1)S(1)} %compare_convert_fusion, bf16[1,4,640,384]{3,2,1,0:T(8,128)(2,1)} %param.20), kind=kOutput, calls=%fused_computation.18 | convolution fusion | flops 2017460224 | bytes 10359808 | tf_op jit(solution)/shard_map/esd,esf->edf/dot_general | solution.py:363
  235.1 0.0 copy-done.10
  235.1 0.0 copy-start.4
  235.1 0.0 copy-start.1
  235.1 7.6 %convert_bitcast_fusion.1 = bf16[1,4,1024,384]{3,2,1,0:T(8,128)(2,1)} fusion(bf16[1,4,640,1024]{3,2,1,0:T(8,128)(2,1)} %param.18, bf16[4,640]{1,0:T(4,128)(2,1)S(1)} %compare_convert_fusion, bf16[1,4,640,384]{3,2,1,0:T(8,128)(2,1)S(1)} %copy-done.10), kind=kOutput, calls=%fused_computation.19 | convolution fusion | flops 2017460224 | bytes 10359808 | tf_op jit(solution)/shard_map/esd,esf->edf/dot_general | solution.py:360
  242.7 0.0 copy-done.4
  242.7 0.8 copy.56
  243.5 0.0 copy-done.1
  (8 shorter events, 0.1 us)
Async XLA Ops:
  0.6 94.6 %copy-start = (bf16[1,4,1024,384]{3,2,1,0:T(8,128)(2,1)S(1)}, bf16[1,4,1024,384]{3,2,1,0:T(8,128)(2,1)}, u32[]{:S(2)}) copy-start(bf16[1,4,1024,384]{3,2,1,0:T(8,128)(2,1)} %param.15) | copy-start | bytes 9437188
  95.3 2.9 %copy-start.9 = (bf16[1,4,1024,384]{3,2,1,0:T(8,128)(2,1)S(1)}, bf16[1,4,1024,384]{3,2,1,0:T(8,128)(2,1)}, u32[]{:S(2)}) copy-start(bf16[1,4,1024,384]{3,2,1,0:T(8,128)(2,1)} %param.16) | copy-start | bytes 9437188
  98.2 14.6 %copy-start.11 = (f32[4,640,384]{1,2,0:T(8,128)}, f32[4,640,384]{1,2,0:T(8,128)S(1)}, u32[]{:S(2)}) copy-start(f32[4,640,384]{1,2,0:T(8,128)S(1)} %fusion.5) | copy-start | bytes 11796484
  98.2 4.9 %copy-start.5 = (bf16[8,256,1024]{2,1,0:T(8,128)(2,1)S(1)}, bf16[8,256,1024]{2,1,0:T(8,128)(2,1)}, u32[]{:S(2)}) copy-start(bf16[8,256,1024]{2,1,0:T(8,128)(2,1)} %get-tuple-element.10) | copy-start | bytes 12582916
  104.6 1.9 copy-start.8
  145.0 81.0 %copy-start.6 = (s32[1,256,8]{1,2,0:T(8,128)S(1)}, s32[1,256,8]{1,2,0:T(8,128)}, u32[]{:S(2)}) copy-start(s32[1,256,8]{1,2,0:T(8,128)} %param.13) | copy-start | bytes 24580
  145.0 81.6 %copy-start.7 = (s32[1,4,8]{2,1,0:T(4,128)S(1)}, s32[1,4,8]{2,1,0:T(4,128)}, u32[]{:S(2)}) copy-start(s32[1,4,8]{2,1,0:T(4,128)} %param.21) | copy-start | bytes 388
  145.6 2.2 copy-start.2
  225.2 0.8 copy-start.3
  226.9 8.2 %copy-start.10 = (bf16[1,4,640,384]{3,2,1,0:T(8,128)(2,1)S(1)}, bf16[1,4,640,384]{3,2,1,0:T(8,128)(2,1)}, u32[]{:S(2)}) copy-start(bf16[1,4,640,384]{3,2,1,0:T(8,128)(2,1)} %param.19) | copy-start | bytes 5898244
  235.1 7.6 %copy-start.4 = (bf16[256,1024]{1,0:T(8,128)(2,1)S(1)}, bf16[256,1024]{1,0:T(8,128)(2,1)}, u32[]{:S(2)}) copy-start(bf16[256,1024]{1,0:T(8,128)(2,1)} %copy-done.3) | copy-start | bytes 1572868
  235.1 8.4 %copy-start.1 = (bf16[1,4,1024,384]{3,2,1,0:T(8,128)(2,1)S(1)}, bf16[1,4,1024,384]{3,2,1,0:T(8,128)(2,1)}, u32[]{:S(2)}) copy-start(bf16[1,4,1024,384]{3,2,1,0:T(8,128)(2,1)} %param.15) | copy-start | bytes 9437188

commit v4 on v3

--- a/solution.py
+++ b/solution.py
@@ -59,7 +59,27 @@
     return 12 * (line - 1) + 3 + (count - 1)
 
 
-def gather_kernel(count, g, x, s, g_all, x_all, s_all, local, send, recv):
+def weight_tile(live, held, saved, outs, expert):
+    mask = live[expert][:, :1]
+    grads = [ref[expert] * mask for ref in saved]
+    tile = 256
+
+    def body(at, carry):
+        columns = pl.ds(pl.multiple_of(at * tile, tile), tile)
+        rows = held[expert, :, columns]
+        for grad, out in zip(grads, outs):
+            out[expert, columns, :] = lax.dot_general(
+                rows, grad, (((0,), (0,)), ((), ())), preferred_element_type=F32
+            ).astype(BF16)
+        return carry
+
+    lax.fori_loop(0, held.shape[2] // tile, body, 0)
+
+
+def gather_kernel(
+    count, g, x, s, live, held_in, gate_in, up_in, g_all, x_all, s_all, gate_out, up_out, held,
+    gate_held, up_held, local, send, recv,
+):
     me, outer, inner, line, sides, partner = place_of(count)
     width = g.shape[1]
     cut = max(width * 3 // 1024, 1) * 128
@@ -69,7 +89,11 @@
         pltpu.make_async_copy(x, x_all.at[me], local.at[1]),
         pltpu.make_async_copy(s, s_all.at[me], local.at[2]),
     ]
-    for copy in own:
+    loads = [
+        pltpu.make_async_copy(src, dst, local.at[3 + at])
+        for at, (src, dst) in enumerate(((held_in, held), (gate_in, gate_held), (up_in, up_held)))
+    ]
+    for copy in own + loads:
         copy.start()
     barrier = pltpu.get_barrier_semaphore()
     for away in range(1, count):
@@ -114,6 +138,15 @@
     ]
     for away in range(1, count):
         late.append((copies.start(s, s_all.at[me], (me + away) % count), None))
+    experts = list(range(held.shape[0]))
+    for copy in loads:
+        copy.wait()
+
+    def work():
+        if experts:
+            weight_tile(live, held, (gate_held, up_held), (gate_out, up_out), experts.pop(0))
+
+    work()
     g_across.wait_recv()
     for side in side_list:
         now[3, side] = hop(None, g_all, few, 0, side, other)
@@ -130,6 +163,10 @@
                     got = all_ref.at[block(step + 1, side) * 2 + inner, :, columns]
                     has = arrives(step, side)
                     late.append((copies.start(got, got, partner, has), has))
+            if at % 2 == 1:
+                work()
+    while experts:
+        work()
     for copy, when in late:
         guarded(when, copy.wait_recv)
     copies.finish()
@@ -137,20 +174,27 @@
         copy.wait()
 
 
-def gather_tokens(count, g, x, s):
+def gather_tokens(count, g, x, s, live, held, gate, up):
     pairs = gather_copies(count)
+    grads = jax.ShapeDtypeStruct((held.shape[0], held.shape[2], gate.shape[2]), BF16)
     return pl.pallas_call(
         functools.partial(gather_kernel, count),
-        out_shape=[jax.ShapeDtypeStruct((count,) + a.shape, a.dtype) for a in (g, x, s)],
-        in_specs=[VMEM] * 3,
-        out_specs=[ANY] * 3,
+        out_shape=[jax.ShapeDtypeStruct((count,) + a.shape, a.dtype) for a in (g, x, s)]
+        + [grads, grads],
+        in_specs=[VMEM] * 4 + [ANY] * 3,
+        out_specs=[ANY] * 3 + [VMEM] * 2,
         scratch_shapes=[
-            pltpu.SemaphoreType.DMA((3,)),
+            pltpu.VMEM(held.shape, BF16),
+            pltpu.VMEM(gate.shape, BF16),
+            pltpu.VMEM(up.shape, BF16),
+            pltpu.SemaphoreType.DMA((6,)),
             pltpu.SemaphoreType.DMA((pairs,)),
             pltpu.SemaphoreType.DMA((pairs,)),
         ],
-        compiler_params=pltpu.CompilerParams(collective_id=0, has_side_effects=True),
-    )(g, x, s)
+        compiler_params=pltpu.CompilerParams(
+            collective_id=0, has_side_effects=True, vmem_limit_bytes=48 * 1024 * 1024
+        ),
+    )(g, x, s, live, held, gate, up)
 
 
 def scatter_copies(count):
@@ -351,18 +395,20 @@
     width = output_grad.shape[2]
 
     small = jnp.concatenate([expert_ids[0].astype(BF16), route_probs[0]], axis=1).T
-    grad_all, input_all, small_all = gather_tokens(
-        ep_count, output_grad[0], layer_input[0], small
+    live = jnp.arange(capacity, dtype=jnp.int32)[None, None, :] < saved_counts[0][:, :, None]
+    live = jnp.broadcast_to(
+        live.reshape(local_experts, slots_all, 1).astype(BF16), (local_experts, slots_all, 128)
     )
-
-    live = jnp.arange(capacity, dtype=jnp.int32)[None, None, :] < saved_counts[0][:, :, None]
-    masked = saved_inputs[0] * live.reshape(local_experts, slots_all).astype(BF16)[:, :, None]
-    gate_part = jnp.einsum(
-        "esd,esf->edf", masked, saved_gate_grad[0], preferred_element_type=F32
-    ).astype(BF16)
-    up_part = jnp.einsum(
-        "esd,esf->edf", masked, saved_up_grad[0], preferred_element_type=F32
-    ).astype(BF16)
+    grad_all, input_all, small_all, gate_part, up_part = gather_tokens(
+        ep_count,
+        output_grad[0],
+        layer_input[0],
+        small,
+        live,
+        saved_inputs[0],
+        saved_gate_grad[0],
+        saved_up_grad[0],
+    )
 
     ids_all = small_all[:, :top_count].astype(jnp.int32)
     probs_all = small_all[:, top_count:].astype(F32)

time: 244 us -> 239 us (0.980)
  matrix products: 64.4 us -> 48.5 us
  local copies, waits for them, and re-layouts: 10.3 us -> 21.6 us
    dot_general x2 -> x0, matrix products: 15.8 us -> none  [the longest x1 8.2 us: per_device(): jnp.einsum('esd,esf->edf', masked, saved_up_grad[0], preferred_element_ty...]
    unnamed x25 -> x29, local copies, waits for them, and re-layouts: 4.76 us -> 14.8 us
where the time goes in v4:
time: 239 us
  Pallas kernels  165 us (69%)
  matrix products  48.5 us (20%)
  local copies, waits for them, and re-layouts  21.6 us (9%)
  other arithmetic  3.1 us (1%)
    pallas_call x1, Pallas kernels, gather_tokens(): pl.pallas_call(functools.partial(gather_kernel, count), out_shape=[jax.Sh...  88 us
    pallas_call x1, Pallas kernels, scatter_tokens(): pl.pallas_call(functools.partial(scatter_kernel, count, sections), out_sh...  76.6 us
    unnamed x29, local copies, waits for them, and re-layouts  14.8 us
    dot_general x1, matrix products, per_device(): jnp.einsum('epf,edf->epd', up_grad, w_up, preferred_element_type=F32)  13 us
    dot_general x1, matrix products, per_device(): jnp.einsum('epf,edf->epd', gate_grad, w_gate, preferred_element_type=F32)  11.2 us
    dot_general x1, matrix products, per_device(): jnp.einsum('epd,efd->epf', grad_part, w_down, preferred_element_type=F32)  6.27 us
    dot_general x2, matrix products, spread(): jnp.einsum('spt,std->spd', pick, tokens, preferred_element_type=F32)  5.26 us
    dot_general x1, matrix products, per_device(): jnp.einsum('epd,edf->epf', input_part, w_up, preferred_element_type=F32)  4.85 us

profile of v4, /device:TPU:9, one launch (start us, length us, event | category | flops | bytes accessed | tf_op | source)
XLA Modules:
  0.0 238.7 jit_solution(17428005532707007544)
XLA Ops:
  0.6 0.0 copy-start
  0.6 0.9 lt.30
  1.5 0.1 lt.31
  1.6 0.1 lt.27
  1.7 0.4 broadcast_in_dim.72.live
  2.1 0.7 bitcast_convert_fusion.1
  2.8 0.7 maximum_bitcast_fusion.s
  3.5 0.0 copy-start.3
  3.5 1.5 copy-done.3
  5.1 0.0 copy-start.4
  5.1 1.5 copy-done.4
  6.6 0.0 copy-start.5
  6.6 1.0 copy-done.5
  7.7 0.0 copy-start.6
  7.7 1.0 copy-done.6
  8.7 88.0 %shard_map.138 = (bf16[8,256,1024]{2,1,0:T(8,128)(2,1)}, bf16[8,256,1024]{2,1,0:T(8,128)(2,1)}, bf16[8,16,256]{2,1,0:T(8,128)(2,1)S(1)}, bf16[4,1024,384]{2,1,0:T(8,128)(2,1)}, bf16[4,1024,384]{2,1,0:T(8,128)(2,1)}) custom-call(bf16[256,1024]{1,0:T(8,128)(2,1)S(1)} %bitcast.69, bf16[256,1024]{1,0:T(8,128)(2,1)S(1)} %bitcast.70, ...), custom_call_target="tpu_custom_call" | custom-call | tf_op jit(solution)/shard_map/pallas_call | solution.py:180
  96.7 0.2 compare_reduce_fusion
  96.9 0.2 fusion.14
  97.2 0.1 eq.57
  97.3 0.4 bitcast_compare_fusion
  97.7 3.7 %convolution_convert_fusion = bf16[8,320,1024]{2,1,0:T(8,128)(2,1)S(1)} fusion(pred[8,320,256]{2,1,0:T(32,128)(4,1)S(1)} %bitcast_compare_fusion, bf16[8,256,1024]{2,1,0:T(8,128)(2,1)} %get-tuple-element.13), kind=kOutput, calls=%fused_computation.15 | convolution fusion | flops 1344798720 | bytes 10092544 | tf_op jit(solution)/shard_map/spt,std->spd/dot_general | solution.py:428
  101.5 0.9 copy.28
  102.4 0.0 copy-done
  102.4 0.0 copy-start.11
  102.4 2.8 %fusion.3 = f32[4,640,384]{1,2,0:T(8,128)S(1)} fusion(bf16[4,640,1024]{2,1,0:T(8,128)(2,1)S(1)} %bitcast.79, bf16[1,4,1024,384]{3,2,1,0:T(8,128)(2,1)S(1)} %copy-done), kind=kOutput, calls=%fused_computation.8 | convolution fusion | flops 2013265920 | bytes 12320768 | tf_op jit(solution)/shard_map/epd,edf->epf/dot_general | solution.py:435
  105.3 0.0 copy-done.11
  105.3 0.0 copy-start.12
  105.3 0.0 copy-start.7
  105.3 4.9 %fusion.6 = f32[4,640,384]{1,2,0:T(8,128)} fusion(bf16[4,640,1024]{2,1,0:T(8,128)(2,1)S(1)} %bitcast.80, bf16[1,4,1024,384]{3,2,1,0:T(8,128)(2,1)S(1)} %copy-done.11), kind=kOutput, calls=%fused_computation.11 | convolution fusion | flops 2013265920 | bytes 12320768 | tf_op jit(solution)/shard_map/epd,edf->epf/dot_general | solution.py:436
  110.1 0.0 copy-done.7
  110.1 1.5 convolution_convert_fusion.1
  111.7 0.0 copy-start.10
  111.7 0.9 copy.27
  112.6 0.9 copy-done.10
  113.6 6.3 %multiply_reduce_fusion = (bf16[4,640]{1,0:T(4,128)(2,1)S(1)}, f32[4,640,384]{1,2,0:T(8,128)}) fusion(f32[4,640,384]{1,2,0:T(8,128)} %fusion.6, f32[4,640,384]{1,2,0:T(8,128)S(1)} %fusion.3, bf16[4,640,1024]{2,1,0:T(8,128)(2,1)S(1)} %bitcast.77, bf16[1,4,384,1024]{3,2,1,0:T(8,128)(2,1)S(1)} %copy-done.10), kind=kOutput, calls=%fused_computation.1 | convolution fusion | flops 2020144640 | bytes 20190208 | tf_op jit(solution)/shard_map/epd,efd->epf/dot_general | solution.py:440
  119.9 0.0 copy-done.12
  119.9 11.2 %fusion.1 = f32[4,640,1024]{2,1,0:T(8,128)} fusion(bf16[1,4,1024,384]{3,2,1,0:T(8,128)(2,1)S(1)} %copy-done, f32[4,640,384]{1,2,0:T(8,128)S(1)} %fusion.3, f32[4,640,384]{1,2,0:T(8,128)} %get-tuple-element.21, f32[4,640,384]{1,2,0:T(8,128)} %fusion.6), kind=kOutput, calls=%fused_computation.6 | convolution fusion | flops 2023096320 | bytes 25427968 | tf_op jit(solution)/shard_map/epf,edf->epd/dot_general | solution.py:444
  131.1 13.0 %add_convert_fusion = bf16[4,640,1024]{2,1,0:T(8,128)(2,1)} fusion(f32[4,640,1024]{2,1,0:T(8,128)} %fusion.1, bf16[1,4,1024,384]{3,2,1,0:T(8,128)(2,1)} %param.16, f32[4,640,384]{1,2,0:T(8,128)} %get-tuple-element.21, f32[4,640,384]{1,2,0:T(8,128)} %copy-done.12), kind=kOutput, calls=%fused_computation | convolution fusion | flops 2024407040 | bytes 26738688 | tf_op jit(solution)/shard_map/epf,edf->epd/dot_general | solution.py:445
  144.1 3.2 %copy.33 = bf16[8,4,80,1024]{3,2,1,0:T(8,128)(2,1)S(1)} copy(bf16[8,4,80,1024]{3,2,0,1:T(8,128)(2,1)} %bitcast.78) | data formatting | bytes 10485760 | tf_op jit(solution)/shard_map/transpose | solution.py:447
  147.3 0.2 fusion.16
  147.5 0.3 fusion.10
  147.8 4.3 %convolution_convert_fusion.2.part = bf16[8,256,1024]{2,1,0:T(8,128)(2,1)} fusion(bf16[8,320,256]{2,1,0:T(8,128)(2,1)S(1)} %fusion.10, bf16[8,320,1024]{2,1,0:T(8,128)(2,1)S(1)} %bitcast.73), kind=kOutput, calls=%fused_computation.17 | convolution fusion | flops 1344274432 | bytes 10747904 | tf_op jit(solution)/shard_map/spt,spd->std/dot_general | solution.py:448
  152.1 0.0 copy-start.9
  152.1 0.1 reshape.94
  152.2 0.5 fusion.11
  152.7 0.0 copy-start.2
  152.7 2.2 copy-done.2
  154.9 76.6 %shard_map.139 = (bf16[256,1024]{1,0:T(8,128)(2,1)S(1)}, bf16[8,4,256]{2,1,0:T(4,128)(2,1)S(1)}) custom-call(bf16[8,256,1024]{2,1,0:T(8,128)(2,1)S(1)} %copy-done.2, bf16[8,4,256]{2,1,0:T(4,128)(2,1)S(1)} %bitcast.72), custom_call_target="tpu_custom_call" | custom-call | tf_op jit(solution)/shard_map/pallas_call | solution.py:341
  231.5 0.0 copy-start.8
  231.5 0.0 copy-done.9
  231.6 0.6 select_reduce_fusion
  232.2 0.8 copy.52
  233.0 0.0 copy-start.1
  233.0 4.0 %copy.53 = bf16[1,4,1024,384]{3,2,1,0:T(8,128)(2,1)} copy(bf16[1,4,1024,384]{3,2,1,0:T(8,128)(2,1)} %bitcast.82) | data formatting | bytes 6291456
  237.0 0.0 copy-done.8
  237.0 1.7 copy.54
  238.7 0.0 copy-done.1
  (9 shorter events, 0.1 us)
Async XLA Ops:
  0.6 101.8 %copy-start = (bf16[1,4,1024,384]{3,2,1,0:T(8,128)(2,1)S(1)}, bf16[1,4,1024,384]{3,2,1,0:T(8,128)(2,1)}, u32[]{:S(2)}) copy-start(bf16[1,4,1024,384]{3,2,1,0:T(8,128)(2,1)} %param.15) | copy-start | bytes 9437188
  3.5 1.5 copy-start.3
  5.1 1.5 copy-start.4
  6.6 1.0 copy-start.5
  7.7 1.0 copy-start.6
  102.4 2.9 %copy-start.11 = (bf16[1,4,1024,384]{3,2,1,0:T(8,128)(2,1)S(1)}, bf16[1,4,1024,384]{3,2,1,0:T(8,128)(2,1)}, u32[]{:S(2)}) copy-start(bf16[1,4,1024,384]{3,2,1,0:T(8,128)(2,1)} %param.16) | copy-start | bytes 9437188
  105.3 14.6 %copy-start.12 = (f32[4,640,384]{1,2,0:T(8,128)}, f32[4,640,384]{1,2,0:T(8,128)S(1)}, u32[]{:S(2)}) copy-start(f32[4,640,384]{1,2,0:T(8,128)S(1)} %fusion.3) | copy-start | bytes 11796484
  105.3 4.9 %copy-start.7 = (bf16[8,256,1024]{2,1,0:T(8,128)(2,1)S(1)}, bf16[8,256,1024]{2,1,0:T(8,128)(2,1)}, u32[]{:S(2)}) copy-start(bf16[8,256,1024]{2,1,0:T(8,128)(2,1)} %get-tuple-element.12) | copy-start | bytes 12582916
  111.7 1.9 copy-start.10
  152.1 79.4 %copy-start.9 = (s32[1,256,8]{1,2,0:T(8,128)S(1)}, s32[1,256,8]{1,2,0:T(8,128)}, u32[]{:S(2)}) copy-start(s32[1,256,8]{1,2,0:T(8,128)} %param.13) | copy-start | bytes 24580
  152.7 2.2 copy-start.2
  231.5 5.5 %copy-start.8 = (bf16[4,1024,384]{2,1,0:T(8,128)(2,1)S(1)}, bf16[4,1024,384]{2,1,0:T(8,128)(2,1)}, u32[]{:S(2)}) copy-start(bf16[4,1024,384]{2,1,0:T(8,128)(2,1)} %get-tuple-element.17) | copy-start | bytes 9437188
  233.0 5.7 %copy-start.1 = (bf16[1,4,1024,384]{3,2,1,0:T(8,128)(2,1)S(1)}, bf16[1,4,1024,384]{3,2,1,0:T(8,128)(2,1)}, u32[]{:S(2)}) copy-start(bf16[1,4,1024,384]{3,2,1,0:T(8,128)(2,1)} %param.15) | copy-start | bytes 9437188
